TPU v7x, 512 devices: a whole 4x4x16 slice. The times are simulated.
512 devices in a mesh: blk: 32 (over z, y_hi), grp: 16 (over x, y_lo, core).
Axes of the slice: x: 4, y: 4 (y_hi: 2, y_lo: 2; y = y_hi * 2 + y_lo), z: 16, core: 2. Of those that a mesh axis runs over, the one named last changes fastest.
Arguments:
- embeddings: bfloat16 [65536, 1024], P(('blk', 'grp')), may hold values from -100 to 100
- labels: int32 [65536], P(('blk', 'grp')), may hold values from 0 to 66439, as said below
Outputs:
- anchor_loss: float32 [16384], P(('blk', 'grp'))
- mean_loss: float32 [], replicated
Inputs may be any that keep to these rules, and one draw needn't show every extreme that they name: `labels`: A label of 1000 or more belongs to one sample only.
All inputs are finite; a program needn't handle non-finite values.
Results may differ from a plain program's by a relative error of at most 0.0003.
Values may be sent and summed in bfloat16 or wider, within the bound.
No kernel may reach another device: no remote copies, remote signals or barrier semaphores. Data moves between devices by JAX's collectives and lax.ppermute only.
A program may use at most 64 MiB of HBM per device.

v0:
```python
import jax
import jax.numpy as jnp
from jax import lax
from jax.experimental import pallas as pl
from jax.experimental.pallas import tpu as pltpu
from jax.sharding import Mesh
from jax.sharding import PartitionSpec as P

D = 1024
A_DEV = 32
KEYS = 128
LAB = 8
X = 4
Y = 4
Z = 16
ROWS = KEYS + LAB
SIDE = A_DEV + LAB
F32 = jnp.float32
BF16 = jnp.bfloat16


def device_at(z, x, y, c):
    return ((((z % Z) * 2 + (y % Y) // 2) * X + x % X) * 2 + y % 2) * 2 + c


SPOTS = [(z, x, y, c) for z in range(Z) for x in range(X) for y in range(Y) for c in range(2)]
LINES = [[device_at(z, k, y, 0) for k in range(X)] for z in range(Z) for y in range(Y)] + [
    [device_at(z, x, k, 1) for k in range(Y)] for z in range(Z) for x in range(X)
]
COLUMNS = [
    [device_at(z, x, y, c) for z in range(Z)] for x in range(X) for y in range(Y) for c in range(2)
]
PLANES = [
    [device_at(z, x, y, c) for x in range(X) for y in range(Y) for c in range(2)] for z in range(Z)
]


def moved(block, target):
    return lax.ppermute(block, "d", [(device_at(*spot), device_at(*target(*spot))) for spot in SPOTS])


def along_z(block, step):
    return moved(block, lambda z, x, y, c: (z + step, x, y, c))


def split_along_z(block, step):
    return moved(block, lambda z, x, y, c: (z + step - 2 * step * c, x, y, c))


def across_lines(block, step):
    return moved(
        block, lambda z, x, y, c: (z, x, y + step, c) if c == 0 else (z, x + step, y, c)
    )


def other_core(block):
    return moved(block, lambda z, x, y, c: (z, x, y, 1 - c))


def swapped_to_all(blocks, groups):
    return lax.all_to_all(blocks, "d", 0, 0, tiled=True, axis_index_groups=groups)


def vmem():
    return pl.BlockSpec(memory_space=pltpu.VMEM)


def smem():
    return pl.BlockSpec(memory_space=pltpu.SMEM)


def call(body, n_in, outs, scratch=(), limit=8):
    return pl.pallas_call(
        body,
        in_specs=[smem()] + [vmem()] * n_in,
        out_specs=jax.tree.map(lambda _: vmem(), outs),
        out_shape=outs,
        scratch_shapes=list(scratch),
        compiler_params=pltpu.CompilerParams(vmem_limit_bytes=limit * 1024 * 1024),
    )


def prepare_body(at, emb, labels, keys, anchors):
    values = emb[...].astype(F32)
    scale = lax.rsqrt(jnp.sum(values * values, axis=1, keepdims=True) + 1e-06)
    unit = (values * scale).astype(BF16)
    for k in range(4):
        keys[k, :KEYS, :] = unit
    anchors[:A_DEV, :] = unit[:A_DEV]
    label = jnp.broadcast_to(labels[...], (8, KEYS))
    high = (label + 256) >> 9
    low = label - high * 512
    top = lax.broadcasted_iota(jnp.int32, (8, KEYS), 0) == 0
    lane = lax.broadcasted_iota(jnp.int32, (8, KEYS), 1)
    blank = jnp.zeros((8, D - 2 * KEYS), BF16)
    for k in range(4):
        keys[k, KEYS:, 2 * KEYS :] = blank
    anchors[A_DEV:, 2 * KEYS :] = blank
    for k, digit in enumerate((high, low)):
        digit = jnp.where(top, digit.astype(F32), 0.0)
        for copy in range(4):
            keys[copy, KEYS:, k * KEYS : (k + 1) * KEYS] = digit.astype(BF16)
        mine = pltpu.roll(jnp.where(lane < A_DEV, digit, 0.0), at[0] * A_DEV, 1)
        anchors[A_DEV:, k * KEYS : (k + 1) * KEYS] = mine.astype(BF16)


def pair_body(at, own, across, pair):
    pair[:A_DEV, :] = own[:A_DEV, :]
    pair[A_DEV : 2 * A_DEV, :] = across[:A_DEV, :]
    tail = own[A_DEV:, :].astype(F32) + across[A_DEV:, :].astype(F32)
    pair[2 * A_DEV :, :] = tail.astype(BF16)


def far_body(at, pair, other, far):
    zh, c = at[0], at[3]
    for step, ref, k in ((0, pair, 0), (2, pair, 1), (3 + 2 * c, other, 0), (1 + 2 * c, other, 1)):
        slot = (zh + step) % 4
        block = ref[k * A_DEV : (k + 1) * A_DEV, :]
        far[pl.ds(pl.multiple_of(slot * A_DEV, A_DEV), A_DEV), :] = block
    tail = pair[2 * A_DEV :, :].astype(F32) + other[2 * A_DEV :, :].astype(F32)
    far[KEYS:, :] = tail.astype(BF16)


def anchors_body(at, far, ahead, across, behind, anchors):
    row = lax.broadcasted_iota(jnp.int32, (LAB, D), 0)
    tail = jnp.zeros((LAB, D), F32)
    for d, ref in enumerate((far, ahead, across, behind)):
        anchors[d * KEYS : (d + 1) * KEYS, :] = ref[:KEYS, :]
        label = jnp.broadcast_to(ref[KEYS:, :].astype(F32)[:1], (LAB, D))
        tail = jnp.where(row == d, label, tail)
    anchors[4 * KEYS :, :] = tail.astype(BF16)


def label_of(rows):
    rows = rows.astype(F32)
    return rows[:, :KEYS] * 512.0 + rows[:, KEYS : 2 * KEYS]


def scores_of(at, keys, anchors, totals, has_own):
    n = KEYS
    labels = label_of(anchors[4 * n :, :])
    if has_own:
        row = lax.broadcasted_iota(jnp.int32, (n, n), 0)
        lane = lax.broadcasted_iota(jnp.int32, (n, n), 1)
        diagonal = (row < A_DEV) & (row + at[0] * A_DEV == lane)

    def product(p, half):
        rows = keys[p][2 * half : 2 * half + 2, :n, :].reshape(2 * n, D)
        return lax.dot_general(
            rows, anchors[: 4 * n, :], (((1,), (1,)), ((), ())), preferred_element_type=F32
        )

    order = [(p, half) for p in range(4) for half in range(2)]
    following = product(*order[0])
    for k, (p, half) in enumerate(order):
        raw = following
        if k + 1 < len(order):
            following = product(*order[k + 1])
        for b in range(2):
            key_label = label_of(keys[p][2 * half + b, n:, :])[:1]
            key_label = jnp.broadcast_to(key_label, (n, n)).T
            for d in range(4):
                dots = raw[b * n : (b + 1) * n, d * n : (d + 1) * n]
                expo = jnp.exp(dots * 10.0 - 10.0)
                positive = key_label == labels[d : d + 1]
                if has_own and p == 0 and d == 0:
                    itself = diagonal & (at[2] == 2 * half + b)
                    expo = jnp.where(itself, 0.0, expo)
                    positive = positive & jnp.logical_not(itself)
                parts = (expo, jnp.where(positive, dots, 0.0), jnp.where(positive, 1.0, 0.0))
                for m, part in enumerate(parts):
                    totals[d][m] += part.reshape(n // 8, 8, n).sum(axis=0)


def mine_body(at, line, plus, minus, two, anchors, out):
    totals = [[jnp.zeros((8, KEYS), F32) for _ in range(3)] for _ in range(4)]
    scores_of(at, (line, plus, minus, two), anchors, totals, True)
    for d in range(4):
        for k in range(3):
            out[d, k] = totals[d][k]


def theirs_body(at, line, plus, minus, two, anchors, before, out):
    totals = [[before[d, k] for k in range(3)] for d in range(4)]
    scores_of(at, (line, plus, minus, two), anchors, totals, False)
    for d in range(4):
        slot = (at[1] + d) % 4
        for k in range(3):
            row = jnp.sum(totals[d][k], axis=0, keepdims=True)
            if k == 1:
                row = row * 10.0
            for z in range(Z):
                out[z, k, pl.ds(slot, 1), :] = row


def loss_body(at, arrived, own, both):
    zh, zl = at[0], at[1]
    total = arrived[0]
    for z in range(1, Z):
        total = total + arrived[z]
    denom, pos_sum, count = total[0], total[1], total[2]
    valid = count > 0.0
    loss = jnp.where(valid, jnp.log(denom) + 10.0 - pos_sum / jnp.maximum(count, 1.0), 0.0)
    classes = lax.broadcasted_iota(jnp.int32, loss.shape, 0)
    mine = jnp.sum(jnp.where(classes == zl, loss, 0.0), axis=0, keepdims=True)
    mine = jnp.broadcast_to(mine, (8, KEYS))
    own[...] = pltpu.roll(mine, (4 - zh) % 4 * A_DEV, 1)
    lane = lax.broadcasted_iota(jnp.int32, (1, KEYS), 1)
    loss_sum = jnp.sum(jnp.sum(loss, axis=0, keepdims=True), axis=1, keepdims=True)
    valid_sum = jnp.sum(
        jnp.sum(jnp.where(valid, 1.0, 0.0), axis=0, keepdims=True), axis=1, keepdims=True
    )
    row = jnp.where(lane == 0, loss_sum, jnp.where(lane == 1, valid_sum, 0.0))
    for k in range(2 * X * Y):
        both[k] = row


def loss_of(embeddings, labels):
    device = lax.axis_index("d")
    c = device % 2
    z = device // 32
    x = device // 4 % 4
    y = device // 16 % 2 * 2 + device // 2 % 2
    at = jnp.stack([z // 4, z % 4, jnp.where(c == 0, x, y), c]).astype(jnp.int32)

    own_keys, own_anchors = call(
        prepare_body,
        2,
        (jax.ShapeDtypeStruct((4, ROWS, D), BF16), jax.ShapeDtypeStruct((SIDE, D), BF16)),
    )(at, embeddings, labels.reshape(1, KEYS))

    line = swapped_to_all(own_keys, LINES)
    across = along_z(own_anchors, 8)

    mine = [line]
    for step in (1, -1, 2):
        mine.append(across_lines(line, step))

    two = jax.ShapeDtypeStruct((2 * A_DEV + LAB, D), BF16)
    (pair,) = call(pair_body, 2, (two,))(at, own_anchors, across)
    other_pair = split_along_z(pair, 4)
    (far,) = call(far_body, 2, (jax.ShapeDtypeStruct((ROWS, D), BF16),))(at, pair, other_pair)
    across_near = split_along_z(far, 2)
    behind = along_z(far, 1)
    ahead = along_z(far, -1)

    theirs = []
    for block in mine:
        theirs.append(other_core(block))

    column = jax.ShapeDtypeStruct((4 * KEYS + LAB, D), BF16)
    (anchors,) = call(anchors_body, 4, (column,))(at, far, ahead, across_near, behind)
    (first,) = call(mine_body, 5, (jax.ShapeDtypeStruct((4, 3, 8, KEYS), F32),), (), 16)(
        at, *mine, anchors
    )
    (sums,) = call(
        theirs_body, 6, (jax.ShapeDtypeStruct((Z, 3, 4, KEYS), F32),), (), 16
    )(at, *theirs, anchors, first)
    arrived = swapped_to_all(sums, COLUMNS)
    own_loss, both = call(
        loss_body,
        1,
        (
            jax.ShapeDtypeStruct((8, KEYS), F32),
            jax.ShapeDtypeStruct((2 * X * Y, 1, KEYS), F32),
        ),
    )(at, arrived)
    everyone = swapped_to_all(both, PLANES).sum(axis=0)[0]
    mean_loss = everyone[0] / jnp.maximum(everyone[1], 1.0)
    return (own_loss[0, :A_DEV], mean_loss)


def solution(mesh):
    flat = Mesh(mesh.devices.reshape(512), ("d",))
    placed = (P("d", None), P("d"))
    return jax.shard_map(
        loss_of, mesh=flat, in_specs=placed, out_specs=(P("d"), P()), check_vma=False
    )
```

profile of v0, /device:TPU:1, one launch (start us, length us, event | category | flops | bytes accessed | tf_op | source)
XLA Modules:
  0.0 172.2 jit_solution(1818682748654452623)
XLA Ops:
  0.7 0.1 pad_add_fusion.at
  0.8 0.0 copy-start
  0.8 0.9 copy-done
  1.8 0.0 copy-start.1
  1.8 0.7 copy-done.1
  2.4 0.7 shard_map.41
  3.1 15.2 %all_to_all.15.line = bf16[4,136,1024]{2,1,0:T(8,128)(2,1)S(1)} all-to-all(bf16[4,136,1024]{2,1,0:T(8,128)(2,1)S(1)} %get-tuple-element.6), channel_id=1, replica_groups={{0,4,8,12},{2,6,10,14},{16,20,24,28},{18,22,26,30},{32,36,40,44},{34,38..., dimensions={0} | all-to-all | bytes 2228224 | tf_op jit(solution)/shard_map/all_to_all | solution.py:61
  18.3 2.8 %collective-permute-start.1 = (bf16[4,136,1024]{2,1,0:T(8,128)(2,1)S(1)}, bf16[4,136,1024]{2,1,0:T(8,128)(2,1)S(1)}, u32[]{:S(2)}, u32[]{:S(2)}) collective-permute-start(bf16[4,136,1024]{2,1,0:T(8,128)(2,1)S(1)} %all_to_all.15.line), channel_id=1, source_target_pairs={{0,2},{1,5},{2,16},{3,7},{16,18},{17,21},{18,0},{19,23},{4,6},{5,9... | collective-permute-start | bytes 3342344 | tf_op jit(solution)/shard_map/ppermute | solution.py:39
  21.2 3.7 %collective-permute-start.3 = (bf16[4,136,1024]{2,1,0:T(8,128)(2,1)S(1)}, bf16[4,136,1024]{2,1,0:T(8,128)(2,1)S(1)}, u32[]{:S(2)}, u32[]{:S(2)}) collective-permute-start(bf16[4,136,1024]{2,1,0:T(8,128)(2,1)S(1)} %all_to_all.15.line), channel_id=1, source_target_pairs={{0,18},{1,13},{2,0},{3,15},{16,2},{17,29},{18,16},{19,31},{4,22},{... | collective-permute-start | bytes 3342344 | tf_op jit(solution)/shard_map/ppermute | solution.py:39
  24.8 3.1 %collective-permute-start.5 = (bf16[4,136,1024]{2,1,0:T(8,128)(2,1)S(1)}, bf16[4,136,1024]{2,1,0:T(8,128)(2,1)S(1)}, u32[]{:S(2)}, u32[]{:S(2)}) collective-permute-start(bf16[4,136,1024]{2,1,0:T(8,128)(2,1)S(1)} %all_to_all.15.line), channel_id=1, source_target_pairs={{0,16},{1,9},{2,18},{3,11},{16,0},{17,25},{18,2},{19,27},{4,20},{5... | collective-permute-start | bytes 3342344 | tf_op jit(solution)/shard_map/ppermute | solution.py:39
  28.0 6.5 %collective-permute-start = (bf16[4,136,1024]{2,1,0:T(8,128)(2,1)S(1)}, bf16[4,136,1024]{2,1,0:T(8,128)(2,1)S(1)}, u32[]{:S(2)}, u32[]{:S(2)}) collective-permute-start(bf16[4,136,1024]{2,1,0:T(8,128)(2,1)S(1)} %all_to_all.15.line), channel_id=1, source_target_pairs={{0,1},{1,0},{2,3},{3,2},{16,17},{17,16},{18,19},{19,18},{4,5},{5,4... | collective-permute-start | bytes 3342344 | tf_op jit(solution)/shard_map/ppermute | solution.py:39
  34.5 1.5 collective-permute-done.1.plus
  36.1 20.0 %collective-permute-start.2 = (bf16[4,136,1024]{2,1,0:T(8,128)(2,1)S(1)}, bf16[4,136,1024]{2,1,0:T(8,128)(2,1)S(1)}, u32[]{:S(2)}, u32[]{:S(2)}) collective-permute-start(bf16[4,136,1024]{2,1,0:T(8,128)(2,1)S(1)} %collective-permute-done.1.plus), channel_id=1, source_target_pairs={{0,1},{1,0},{2,3},{3,2},{16,17},{17,16},{18,19},{19,18},{4,5},{5,4... | collective-permute-start | bytes 3342344 | tf_op jit(solution)/shard_map/ppermute | solution.py:39
  56.1 0.0 collective-permute-done.3.minus
  56.1 1.9 %collective-permute-start.4 = (bf16[4,136,1024]{2,1,0:T(8,128)(2,1)S(1)}, bf16[4,136,1024]{2,1,0:T(8,128)(2,1)S(1)}, u32[]{:S(2)}, u32[]{:S(2)}) collective-permute-start(bf16[4,136,1024]{2,1,0:T(8,128)(2,1)S(1)} %collective-permute-done.3.minus), channel_id=1, source_target_pairs={{0,1},{1,0},{2,3},{3,2},{16,17},{17,16},{18,19},{19,18},{4,5},{5,4... | collective-permute-start | bytes 3342344 | tf_op jit(solution)/shard_map/ppermute | solution.py:39
  58.0 0.0 collective-permute-done.5.two
  58.0 2.4 %collective-permute-start.6 = (bf16[4,136,1024]{2,1,0:T(8,128)(2,1)S(1)}, bf16[4,136,1024]{2,1,0:T(8,128)(2,1)S(1)}, u32[]{:S(2)}, u32[]{:S(2)}) collective-permute-start(bf16[4,136,1024]{2,1,0:T(8,128)(2,1)S(1)} %collective-permute-done.5.two), channel_id=1, source_target_pairs={{0,1},{1,0},{2,3},{3,2},{16,17},{17,16},{18,19},{19,18},{4,5},{5,4... | collective-permute-start | bytes 3342344 | tf_op jit(solution)/shard_map/ppermute | solution.py:39
  60.4 8.7 %collective-permute-start.7 = (bf16[40,1024]{1,0:T(8,128)(2,1)S(1)}, bf16[40,1024]{1,0:T(8,128)(2,1)S(1)}, u32[]{:S(2)}, u32[]{:S(2)}) collective-permute-start(bf16[40,1024]{1,0:T(8,128)(2,1)S(1)} %get-tuple-element.7.own), channel_id=1, source_target_pairs={{0,256},{1,257},{2,258},{3,259},{16,272},{17,273},{18,274},{19,275... | collective-permute-start | bytes 245768 | tf_op jit(solution)/shard_map/ppermute | solution.py:39
  69.1 5.9 %collective-permute-done.7.across = bf16[40,1024]{1,0:T(8,128)(2,1)S(1)} collective-permute-done((bf16[40,1024]{1,0:T(8,128)(2,1)S(1)}, bf16[40,1024]{1,0:T(8,128)(2,1)S(1)}, u32[]{:S(2)}, u32[]{:S(2)}) %collective-permute-start.7) | collective-permute-done | bytes 81952 | tf_op jit(solution)/shard_map/ppermute | solution.py:39
  75.0 0.6 shard_map.42.pair
  75.6 5.7 %collective-permute-start.8 = (bf16[72,1024]{1,0:T(8,128)(2,1)S(1)}, bf16[72,1024]{1,0:T(8,128)(2,1)S(1)}, u32[]{:S(2)}, u32[]{:S(2)}) collective-permute-start(bf16[72,1024]{1,0:T(8,128)(2,1)S(1)} %shard_map.42.pair), channel_id=1, source_target_pairs={{0,128},{1,385},{2,130},{3,387},{16,144},{17,401},{18,146},{19,403... | collective-permute-start | bytes 442376 | tf_op jit(solution)/shard_map/ppermute | solution.py:39
  81.3 7.8 %collective-permute-done.8.other = bf16[72,1024]{1,0:T(8,128)(2,1)S(1)} collective-permute-done((bf16[72,1024]{1,0:T(8,128)(2,1)S(1)}, bf16[72,1024]{1,0:T(8,128)(2,1)S(1)}, u32[]{:S(2)}, u32[]{:S(2)}) %collective-permute-start.8) | collective-permute-done | bytes 147488 | tf_op jit(solution)/shard_map/ppermute | solution.py:39
  89.1 0.6 shard_map.43.far
  89.7 7.0 %collective-permute-start.10 = (bf16[136,1024]{1,0:T(8,128)(2,1)S(1)}, bf16[136,1024]{1,0:T(8,128)(2,1)S(1)}, u32[]{:S(2)}, u32[]{:S(2)}) collective-permute-start(bf16[136,1024]{1,0:T(8,128)(2,1)S(1)} %shard_map.43.far), channel_id=1, source_target_pairs={{0,64},{1,449},{2,66},{3,451},{16,80},{17,465},{18,82},{19,467},{4... | collective-permute-start | bytes 835592 | tf_op jit(solution)/shard_map/ppermute | solution.py:39
  96.7 6.4 %collective-permute-done.10.across = bf16[136,1024]{1,0:T(8,128)(2,1)S(1)} collective-permute-done((bf16[136,1024]{1,0:T(8,128)(2,1)S(1)}, bf16[136,1024]{1,0:T(8,128)(2,1)S(1)}, u32[]{:S(2)}, u32[]{:S(2)}) %collective-permute-start.10) | collective-permute-done | bytes 278560 | tf_op jit(solution)/shard_map/ppermute | solution.py:39
  103.1 2.2 %collective-permute-start.11 = (bf16[136,1024]{1,0:T(8,128)(2,1)S(1)}, bf16[136,1024]{1,0:T(8,128)(2,1)S(1)}, u32[]{:S(2)}, u32[]{:S(2)}) collective-permute-start(bf16[136,1024]{1,0:T(8,128)(2,1)S(1)} %shard_map.43.far), channel_id=1, source_target_pairs={{0,32},{1,33},{2,34},{3,35},{16,48},{17,49},{18,50},{19,51},{4,36}... | collective-permute-start | bytes 835592 | tf_op jit(solution)/shard_map/ppermute | solution.py:39
  105.3 6.8 %collective-permute-done.11.behind = bf16[136,1024]{1,0:T(8,128)(2,1)S(1)} collective-permute-done((bf16[136,1024]{1,0:T(8,128)(2,1)S(1)}, bf16[136,1024]{1,0:T(8,128)(2,1)S(1)}, u32[]{:S(2)}, u32[]{:S(2)}) %collective-permute-start.11) | collective-permute-done | bytes 278560 | tf_op jit(solution)/shard_map/ppermute | solution.py:39
  112.1 3.4 %collective-permute-start.9 = (bf16[136,1024]{1,0:T(8,128)(2,1)S(1)}, bf16[136,1024]{1,0:T(8,128)(2,1)S(1)}, u32[]{:S(2)}, u32[]{:S(2)}) collective-permute-start(bf16[136,1024]{1,0:T(8,128)(2,1)S(1)} %shard_map.43.far), channel_id=1, source_target_pairs={{0,480},{1,481},{2,482},{3,483},{16,496},{17,497},{18,498},{19,499... | collective-permute-start | bytes 835592 | tf_op jit(solution)/shard_map/ppermute | solution.py:39
  115.5 3.8 %collective-permute-done.9.ahead = bf16[136,1024]{1,0:T(8,128)(2,1)S(1)} collective-permute-done((bf16[136,1024]{1,0:T(8,128)(2,1)S(1)}, bf16[136,1024]{1,0:T(8,128)(2,1)S(1)}, u32[]{:S(2)}, u32[]{:S(2)}) %collective-permute-start.9) | collective-permute-done | bytes 278560 | tf_op jit(solution)/shard_map/ppermute | solution.py:39
  119.4 0.6 shard_map.44.anchors
  120.0 3.7 %shard_map.45.before = f32[4,3,8,128]{3,2,1,0:T(8,128)S(1)} custom-call(s32[4]{0:T(128)S(1)} %pad_add_fusion.at, bf16[4,136,1024]{2,1,0:T(8,128)(2,1)S(1)} %all_to_all.15.line, bf16[4,136,1024]{2,1,0:T(8,128)(2,1)S(1)} %collective-permute-done.1.plus, bf16[4,136,1024]{2,1,0:T(8,128)(2,1)S(1)} %collective-permute-done.3.minus, ...), custom_call_target="tpu_custom_call" | custom-call | tf_op jit(solution)/shard_map/pallas_call | solution.py:253
  123.7 0.0 collective-permute-done.line
  123.7 0.0 collective-permute-done.2.plus
  123.7 0.0 collective-permute-done.4.minus
  123.7 0.0 collective-permute-done.6.two
  123.7 3.7 %shard_map.46 = f32[16,3,4,128]{3,2,1,0:T(4,128)S(1)} custom-call(s32[4]{0:T(128)S(1)} %pad_add_fusion.at, bf16[4,136,1024]{2,1,0:T(8,128)(2,1)S(1)} %collective-permute-done.line, bf16[4,136,1024]{2,1,0:T(8,128)(2,1)S(1)} %collective-permute-done.2.plus, bf16[4,136,1024]{2,1,0:T(8,128)(2,1)S(1)} %collective-permute-done.4.minus, ...), custom_call_target="tpu_custom_call" | custom-call | tf_op jit(solution)/shard_map/pallas_call | solution.py:256
  127.4 21.6 %all_to_all.16.arrived = f32[16,3,4,128]{3,2,1,0:T(4,128)S(1)} all-to-all(f32[16,3,4,128]{3,2,1,0:T(4,128)S(1)} %shard_map.46), channel_id=1, replica_groups={{0,32,64,96,128,160,192,224,256,288,320,352,384,416,448,480},{1,33,65,9..., dimensions={0} | all-to-all | bytes 196608 | tf_op jit(solution)/shard_map/all_to_all | solution.py:61
  149.0 1.3 shard_map.47
  150.3 12.0 %all-to-all-start.2 = ((f32[32,1,128]{2,1,0:T(1,128)}), f32[32,1,128]{2,1,0:T(1,128)S(1)}, u32[]{:S(2)}, u32[]{:S(2)}) async-start(f32[32,1,128]{2,1,0:T(1,128)} %get-tuple-element.9), calls=%async_computation.2 | async-start | bytes 32768 | tf_op jit(solution)/shard_map/all_to_all | solution.py:61
  162.2 0.5 slice_bitcast_fusion
  162.7 6.4 %all-to-all-done.2 = f32[32,1,128]{2,1,0:T(1,128)S(1)} async-done(((f32[32,1,128]{2,1,0:T(1,128)}), f32[32,1,128]{2,1,0:T(1,128)S(1)}, u32[]{:S(2)}, u32[]{:S(2)}) %all-to-all-start.2) | async-done | bytes 16416 | tf_op jit(solution)/shard_map/all_to_all | solution.py:61
  169.2 0.1 reduce_sum.11
  169.2 0.6 fusion
Async XLA Ops:
  0.8 1.0 copy-start
  1.8 0.7 copy-start.1
  18.3 17.7 %collective-permute-start.1 = (bf16[4,136,1024]{2,1,0:T(8,128)(2,1)S(1)}, bf16[4,136,1024]{2,1,0:T(8,128)(2,1)S(1)}, u32[]{:S(2)}, u32[]{:S(2)}) collective-permute-start(bf16[4,136,1024]{2,1,0:T(8,128)(2,1)S(1)} %all_to_all.15.line), channel_id=1, source_target_pairs={{0,2},{1,5},{2,16},{3,7},{16,18},{17,21},{18,0},{19,23},{4,6},{5,9... | collective-permute-start | bytes 3342344 | tf_op jit(solution)/shard_map/ppermute | solution.py:39
  21.2 34.9 %collective-permute-start.3 = (bf16[4,136,1024]{2,1,0:T(8,128)(2,1)S(1)}, bf16[4,136,1024]{2,1,0:T(8,128)(2,1)S(1)}, u32[]{:S(2)}, u32[]{:S(2)}) collective-permute-start(bf16[4,136,1024]{2,1,0:T(8,128)(2,1)S(1)} %all_to_all.15.line), channel_id=1, source_target_pairs={{0,18},{1,13},{2,0},{3,15},{16,2},{17,29},{18,16},{19,31},{4,22},{... | collective-permute-start | bytes 3342344 | tf_op jit(solution)/shard_map/ppermute | solution.py:39
  24.8 33.2 %collective-permute-start.5 = (bf16[4,136,1024]{2,1,0:T(8,128)(2,1)S(1)}, bf16[4,136,1024]{2,1,0:T(8,128)(2,1)S(1)}, u32[]{:S(2)}, u32[]{:S(2)}) collective-permute-start(bf16[4,136,1024]{2,1,0:T(8,128)(2,1)S(1)} %all_to_all.15.line), channel_id=1, source_target_pairs={{0,16},{1,9},{2,18},{3,11},{16,0},{17,25},{18,2},{19,27},{4,20},{5... | collective-permute-start | bytes 3342344 | tf_op jit(solution)/shard_map/ppermute | solution.py:39
  28.0 95.7 %collective-permute-start = (bf16[4,136,1024]{2,1,0:T(8,128)(2,1)S(1)}, bf16[4,136,1024]{2,1,0:T(8,128)(2,1)S(1)}, u32[]{:S(2)}, u32[]{:S(2)}) collective-permute-start(bf16[4,136,1024]{2,1,0:T(8,128)(2,1)S(1)} %all_to_all.15.line), channel_id=1, source_target_pairs={{0,1},{1,0},{2,3},{3,2},{16,17},{17,16},{18,19},{19,18},{4,5},{5,4... | collective-permute-start | bytes 3342344 | tf_op jit(solution)/shard_map/ppermute | solution.py:39
  36.1 87.6 %collective-permute-start.2 = (bf16[4,136,1024]{2,1,0:T(8,128)(2,1)S(1)}, bf16[4,136,1024]{2,1,0:T(8,128)(2,1)S(1)}, u32[]{:S(2)}, u32[]{:S(2)}) collective-permute-start(bf16[4,136,1024]{2,1,0:T(8,128)(2,1)S(1)} %collective-permute-done.1.plus), channel_id=1, source_target_pairs={{0,1},{1,0},{2,3},{3,2},{16,17},{17,16},{18,19},{19,18},{4,5},{5,4... | collective-permute-start | bytes 3342344 | tf_op jit(solution)/shard_map/ppermute | solution.py:39
  56.1 67.6 %collective-permute-start.4 = (bf16[4,136,1024]{2,1,0:T(8,128)(2,1)S(1)}, bf16[4,136,1024]{2,1,0:T(8,128)(2,1)S(1)}, u32[]{:S(2)}, u32[]{:S(2)}) collective-permute-start(bf16[4,136,1024]{2,1,0:T(8,128)(2,1)S(1)} %collective-permute-done.3.minus), channel_id=1, source_target_pairs={{0,1},{1,0},{2,3},{3,2},{16,17},{17,16},{18,19},{19,18},{4,5},{5,4... | collective-permute-start | bytes 3342344 | tf_op jit(solution)/shard_map/ppermute | solution.py:39
  58.0 65.7 %collective-permute-start.6 = (bf16[4,136,1024]{2,1,0:T(8,128)(2,1)S(1)}, bf16[4,136,1024]{2,1,0:T(8,128)(2,1)S(1)}, u32[]{:S(2)}, u32[]{:S(2)}) collective-permute-start(bf16[4,136,1024]{2,1,0:T(8,128)(2,1)S(1)} %collective-permute-done.5.two), channel_id=1, source_target_pairs={{0,1},{1,0},{2,3},{3,2},{16,17},{17,16},{18,19},{19,18},{4,5},{5,4... | collective-permute-start | bytes 3342344 | tf_op jit(solution)/shard_map/ppermute | solution.py:39
  60.4 14.6 %collective-permute-start.7 = (bf16[40,1024]{1,0:T(8,128)(2,1)S(1)}, bf16[40,1024]{1,0:T(8,128)(2,1)S(1)}, u32[]{:S(2)}, u32[]{:S(2)}) collective-permute-start(bf16[40,1024]{1,0:T(8,128)(2,1)S(1)} %get-tuple-element.7.own), channel_id=1, source_target_pairs={{0,256},{1,257},{2,258},{3,259},{16,272},{17,273},{18,274},{19,275... | collective-permute-start | bytes 245768 | tf_op jit(solution)/shard_map/ppermute | solution.py:39
  75.6 13.5 %collective-permute-start.8 = (bf16[72,1024]{1,0:T(8,128)(2,1)S(1)}, bf16[72,1024]{1,0:T(8,128)(2,1)S(1)}, u32[]{:S(2)}, u32[]{:S(2)}) collective-permute-start(bf16[72,1024]{1,0:T(8,128)(2,1)S(1)} %shard_map.42.pair), channel_id=1, source_target_pairs={{0,128},{1,385},{2,130},{3,387},{16,144},{17,401},{18,146},{19,403... | collective-permute-start | bytes 442376 | tf_op jit(solution)/shard_map/ppermute | solution.py:39
  89.7 13.4 %collective-permute-start.10 = (bf16[136,1024]{1,0:T(8,128)(2,1)S(1)}, bf16[136,1024]{1,0:T(8,128)(2,1)S(1)}, u32[]{:S(2)}, u32[]{:S(2)}) collective-permute-start(bf16[136,1024]{1,0:T(8,128)(2,1)S(1)} %shard_map.43.far), channel_id=1, source_target_pairs={{0,64},{1,449},{2,66},{3,451},{16,80},{17,465},{18,82},{19,467},{4... | collective-permute-start | bytes 835592 | tf_op jit(solution)/shard_map/ppermute | solution.py:39
  103.1 9.0 %collective-permute-start.11 = (bf16[136,1024]{1,0:T(8,128)(2,1)S(1)}, bf16[136,1024]{1,0:T(8,128)(2,1)S(1)}, u32[]{:S(2)}, u32[]{:S(2)}) collective-permute-start(bf16[136,1024]{1,0:T(8,128)(2,1)S(1)} %shard_map.43.far), channel_id=1, source_target_pairs={{0,32},{1,33},{2,34},{3,35},{16,48},{17,49},{18,50},{19,51},{4,36}... | collective-permute-start | bytes 835592 | tf_op jit(solution)/shard_map/ppermute | solution.py:39
  112.1 7.3 %collective-permute-start.9 = (bf16[136,1024]{1,0:T(8,128)(2,1)S(1)}, bf16[136,1024]{1,0:T(8,128)(2,1)S(1)}, u32[]{:S(2)}, u32[]{:S(2)}) collective-permute-start(bf16[136,1024]{1,0:T(8,128)(2,1)S(1)} %shard_map.43.far), channel_id=1, source_target_pairs={{0,480},{1,481},{2,482},{3,483},{16,496},{17,497},{18,498},{19,499... | collective-permute-start | bytes 835592 | tf_op jit(solution)/shard_map/ppermute | solution.py:39
  150.3 18.9 %all-to-all-start.2 = ((f32[32,1,128]{2,1,0:T(1,128)}), f32[32,1,128]{2,1,0:T(1,128)S(1)}, u32[]{:S(2)}, u32[]{:S(2)}) async-start(f32[32,1,128]{2,1,0:T(1,128)} %get-tuple-element.9), calls=%async_computation.2 | async-start | bytes 32768 | tf_op jit(solution)/shard_map/all_to_all | solution.py:61
where the time goes:
time: 173 us; the launch traced here: 172 us
  starting transfers between devices  79.4 us (46%)
  waiting for transfers between devices  38.8 us (22%)
  blocking collectives  36.8 us (21%)
  Pallas kernels  11.1 us (6%)
  between operations  3.37 us (2%)
  local copies, waits for them, and re-layouts  2.71 us (2%)
    ppermute x12, starting transfers between devices, moved(): lax.ppermute(block, 'd', [(device_at(*spot), device_at(*target(*spot))) f...  67.4 us
    all_to_all x2, blocking collectives, swapped_to_all(): lax.all_to_all(blocks, 'd', 0, 0, tiled=True, axis_index_groups=groups)  36.8 us
    ppermute x12, waiting for transfers between devices, moved(): lax.ppermute(block, 'd', [(device_at(*spot), device_at(*target(*spot))) f...  32.4 us
    all_to_all x1, starting transfers between devices, swapped_to_all(): lax.all_to_all(blocks, 'd', 0, 0, tiled=True, axis_index_groups=groups)  12 us
    all_to_all x1, waiting for transfers between devices, swapped_to_all(): lax.all_to_all(blocks, 'd', 0, 0, tiled=True, axis_index_groups=groups)  6.44 us
    pallas_call x1, Pallas kernels, loss_of(): call(theirs_body, 6, (jax.ShapeDtypeStruct((Z, 3, 4, KEYS), F32),), (), 16)  3.68 us
    pallas_call x1, Pallas kernels, loss_of(): call(mine_body, 5, (jax.ShapeDtypeStruct((4, 3, 8, KEYS), F32),), (), 16)  3.67 us
  transfers between devices with their start and end apart: 13, of which 7 were waited for; matrix products, arithmetic and copies ran while one was open for 0% of the time, Pallas kernels for 3%

commit v1 on v0

--- a/solution.py
+++ b/solution.py
@@ -121,6 +121,11 @@
     far[KEYS:, :] = tail.astype(BF16)
 
 
+def rest_body(at, plus, minus, two, rest):
+    for k, ref in enumerate((plus, minus, two)):
+        rest[k] = ref[...]
+
+
 def anchors_body(at, far, ahead, across, behind, anchors):
     row = lax.broadcasted_iota(jnp.int32, (LAB, D), 0)
     tail = jnp.zeros((LAB, D), F32)
@@ -172,17 +177,17 @@
                     totals[d][m] += part.reshape(n // 8, 8, n).sum(axis=0)
 
 
-def mine_body(at, line, plus, minus, two, anchors, out):
+def mine_body(at, line, rest, anchors, out):
     totals = [[jnp.zeros((8, KEYS), F32) for _ in range(3)] for _ in range(4)]
-    scores_of(at, (line, plus, minus, two), anchors, totals, True)
+    scores_of(at, (line, rest.at[0], rest.at[1], rest.at[2]), anchors, totals, True)
     for d in range(4):
         for k in range(3):
             out[d, k] = totals[d][k]
 
 
-def theirs_body(at, line, plus, minus, two, anchors, before, out):
+def theirs_body(at, line, rest, anchors, before, out):
     totals = [[before[d, k] for k in range(3)] for d in range(4)]
-    scores_of(at, (line, plus, minus, two), anchors, totals, False)
+    scores_of(at, (line, rest.at[0], rest.at[1], rest.at[2]), anchors, totals, False)
     for d in range(4):
         slot = (at[1] + d) % 4
         for k in range(3):
@@ -232,9 +237,9 @@
     line = swapped_to_all(own_keys, LINES)
     across = along_z(own_anchors, 8)
 
-    mine = [line]
+    plane = []
     for step in (1, -1, 2):
-        mine.append(across_lines(line, step))
+        plane.append(across_lines(line, step))
 
     two = jax.ShapeDtypeStruct((2 * A_DEV + LAB, D), BF16)
     (pair,) = call(pair_body, 2, (two,))(at, own_anchors, across)
@@ -244,18 +249,18 @@
     behind = along_z(far, 1)
     ahead = along_z(far, -1)
 
-    theirs = []
-    for block in mine:
-        theirs.append(other_core(block))
+    (rest,) = call(rest_body, 3, (jax.ShapeDtypeStruct((3, 4, ROWS, D), BF16),))(at, *plane)
+    other_line = other_core(line)
+    other_rest = other_core(rest)
 
     column = jax.ShapeDtypeStruct((4 * KEYS + LAB, D), BF16)
     (anchors,) = call(anchors_body, 4, (column,))(at, far, ahead, across_near, behind)
-    (first,) = call(mine_body, 5, (jax.ShapeDtypeStruct((4, 3, 8, KEYS), F32),), (), 16)(
-        at, *mine, anchors
+    (first,) = call(mine_body, 3, (jax.ShapeDtypeStruct((4, 3, 8, KEYS), F32),), (), 16)(
+        at, line, rest, anchors
     )
     (sums,) = call(
-        theirs_body, 6, (jax.ShapeDtypeStruct((Z, 3, 4, KEYS), F32),), (), 16
-    )(at, *theirs, anchors, first)
+        theirs_body, 4, (jax.ShapeDtypeStruct((Z, 3, 4, KEYS), F32),), (), 16
+    )(at, other_line, other_rest, anchors, first)
     arrived = swapped_to_all(sums, COLUMNS)
     own_loss, both = call(
         loss_body,
@@ -265,9 +270,10 @@
             jax.ShapeDtypeStruct((2 * X * Y, 1, KEYS), F32),
         ),
     )(at, arrived)
+    anchor_loss, both = lax.optimization_barrier((own_loss[0, :A_DEV], both))
     everyone = swapped_to_all(both, PLANES).sum(axis=0)[0]
     mean_loss = everyone[0] / jnp.maximum(everyone[1], 1.0)
-    return (own_loss[0, :A_DEV], mean_loss)
+    return (anchor_loss, mean_loss)
 
 
 def solution(mesh):

time: 173 us -> 159 us (0.919)
  starting transfers between devices: 79.4 us -> 54.3 us
  blocking collectives: 36.8 us -> 48.5 us
    ppermute x12 -> x10, starting transfers between devices: 67.4 us -> 54.3 us  [moved(): lax.ppermute(block, 'd', [(device_at(*spot), device_at(*target(*spot))) f...]
    all_to_all x1 -> x0, starting transfers between devices: 12 us -> none  [swapped_to_all(): lax.all_to_all(blocks, 'd', 0, 0, tiled=True, axis_index_groups=groups)]
    all_to_all x2 -> x3, blocking collectives: 36.8 us -> 48.5 us  [swapped_to_all(): lax.all_to_all(blocks, 'd', 0, 0, tiled=True, axis_index_groups=groups)]
    all_to_all x1 -> x0, waiting for transfers between devices: 6.44 us -> none  [swapped_to_all(): lax.all_to_all(blocks, 'd', 0, 0, tiled=True, axis_index_groups=groups)]
    ppermute x12 -> x10, waiting for transfers between devices: 32.4 us -> 38 us  [moved(): lax.ppermute(block, 'd', [(device_at(*spot), device_at(*target(*spot))) f...]
    pallas_call x2 -> x3, Pallas kernels: 7.35 us -> 8.11 us  [the longest x1 3.68 us: loss_of(): call(theirs_body, 4, (jax.ShapeDtypeStruct((Z, 3, 4, KEYS), F32),), (), 16)]
  transfers between devices with their start and end apart: 13 -> 10, of which waited for: 7 -> 6; matrix products, arithmetic and copies ran while one was open for 0% -> 0% of each run, Pallas kernels for 3% -> 3%
where the time goes in v1:
time: 159 us; the launch traced here: 158 us
  starting transfers between devices  54.3 us (34%)
  blocking collectives  48.5 us (31%)
  waiting for transfers between devices  38 us (24%)
  Pallas kernels  11.2 us (7%)
  between operations  3.33 us (2%)
  local copies, waits for them, and re-layouts  2.71 us (2%)
    ppermute x10, starting transfers between devices, moved(): lax.ppermute(block, 'd', [(device_at(*spot), device_at(*target(*spot))) f...  54.3 us
    all_to_all x3, blocking collectives, swapped_to_all(): lax.all_to_all(blocks, 'd', 0, 0, tiled=True, axis_index_groups=groups)  48.5 us
    ppermute x10, waiting for transfers between devices, moved(): lax.ppermute(block, 'd', [(device_at(*spot), device_at(*target(*spot))) f...  38 us
    pallas_call x1, Pallas kernels, loss_of(): call(theirs_body, 4, (jax.ShapeDtypeStruct((Z, 3, 4, KEYS), F32),), (), 16)  3.68 us
    pallas_call x1, Pallas kernels, loss_of(): call(mine_body, 3, (jax.ShapeDtypeStruct((4, 3, 8, KEYS), F32),), (), 16)  3.66 us
  transfers between devices with their start and end apart: 10, of which 6 were waited for; matrix products, arithmetic and copies ran while one was open for 0% of the time, Pallas kernels for 3%

profile of v1, /device:TPU:1, one launch (start us, length us, event | category | flops | bytes accessed | tf_op | source)
XLA Modules:
  0.0 158.2 jit_solution(12083586523689447879)
XLA Ops:
  0.7 0.1 pad_add_fusion.at
  0.8 0.0 copy-start
  0.8 0.9 copy-done
  1.8 0.0 copy-start.1
  1.8 0.7 copy-done.1
  2.4 0.7 shard_map.41
  3.1 15.2 %all_to_all.15.line = bf16[4,136,1024]{2,1,0:T(8,128)(2,1)S(1)} all-to-all(bf16[4,136,1024]{2,1,0:T(8,128)(2,1)S(1)} %get-tuple-element.8), channel_id=1, replica_groups={{0,4,8,12},{2,6,10,14},{16,20,24,28},{18,22,26,30},{32,36,40,44},{34,38..., dimensions={0} | all-to-all | bytes 2228224 | tf_op jit(solution)/shard_map/all_to_all | solution.py:61
  18.3 4.3 %collective-permute-start.3 = (bf16[4,136,1024]{2,1,0:T(8,128)(2,1)S(1)}, bf16[4,136,1024]{2,1,0:T(8,128)(2,1)S(1)}, u32[]{:S(2)}, u32[]{:S(2)}) collective-permute-start(bf16[4,136,1024]{2,1,0:T(8,128)(2,1)S(1)} %all_to_all.15.line), channel_id=1, source_target_pairs={{0,16},{1,9},{2,18},{3,11},{16,0},{17,25},{18,2},{19,27},{4,20},{5... | collective-permute-start | bytes 3342344 | tf_op jit(solution)/shard_map/ppermute | solution.py:39
  22.7 2.8 %collective-permute-start.2 = (bf16[4,136,1024]{2,1,0:T(8,128)(2,1)S(1)}, bf16[4,136,1024]{2,1,0:T(8,128)(2,1)S(1)}, u32[]{:S(2)}, u32[]{:S(2)}) collective-permute-start(bf16[4,136,1024]{2,1,0:T(8,128)(2,1)S(1)} %all_to_all.15.line), channel_id=1, source_target_pairs={{0,18},{1,13},{2,0},{3,15},{16,2},{17,29},{18,16},{19,31},{4,22},{... | collective-permute-start | bytes 3342344 | tf_op jit(solution)/shard_map/ppermute | solution.py:39
  25.5 2.5 %collective-permute-start.1 = (bf16[4,136,1024]{2,1,0:T(8,128)(2,1)S(1)}, bf16[4,136,1024]{2,1,0:T(8,128)(2,1)S(1)}, u32[]{:S(2)}, u32[]{:S(2)}) collective-permute-start(bf16[4,136,1024]{2,1,0:T(8,128)(2,1)S(1)} %all_to_all.15.line), channel_id=1, source_target_pairs={{0,2},{1,5},{2,16},{3,7},{16,18},{17,21},{18,0},{19,23},{4,6},{5,9... | collective-permute-start | bytes 3342344 | tf_op jit(solution)/shard_map/ppermute | solution.py:39
  28.0 8.4 %collective-permute-done.3.two = bf16[4,136,1024]{2,1,0:T(8,128)(2,1)S(1)} collective-permute-done((bf16[4,136,1024]{2,1,0:T(8,128)(2,1)S(1)}, bf16[4,136,1024]{2,1,0:T(8,128)(2,1)S(1)}, u32[]{:S(2)}, u32[]{:S(2)}) %collective-permute-start.3) | collective-permute-done | bytes 1114144 | tf_op jit(solution)/shard_map/ppermute | solution.py:39
  36.4 12.0 %collective-permute-done.2.minus = bf16[4,136,1024]{2,1,0:T(8,128)(2,1)S(1)} collective-permute-done((bf16[4,136,1024]{2,1,0:T(8,128)(2,1)S(1)}, bf16[4,136,1024]{2,1,0:T(8,128)(2,1)S(1)}, u32[]{:S(2)}, u32[]{:S(2)}) %collective-permute-start.2) | collective-permute-done | bytes 1114144 | tf_op jit(solution)/shard_map/ppermute | solution.py:39
  48.4 0.0 collective-permute-done.1.plus
  48.4 0.8 shard_map.42.rest
  49.2 7.9 %collective-permute-start.4 = (bf16[3,4,136,1024]{3,2,1,0:T(8,128)(2,1)S(1)}, bf16[3,4,136,1024]{3,2,1,0:T(8,128)(2,1)S(1)}, u32[]{:S(2)}, u32[]{:S(2)}) collective-permute-start(bf16[3,4,136,1024]{3,2,1,0:T(8,128)(2,1)S(1)} %shard_map.42.rest), channel_id=1, source_target_pairs={{0,1},{1,0},{2,3},{3,2},{16,17},{17,16},{18,19},{19,18},{4,5},{5,4... | collective-permute-start | bytes 10027016 | tf_op jit(solution)/shard_map/ppermute | solution.py:39
  57.1 1.9 %collective-permute-start = (bf16[4,136,1024]{2,1,0:T(8,128)(2,1)S(1)}, bf16[4,136,1024]{2,1,0:T(8,128)(2,1)S(1)}, u32[]{:S(2)}, u32[]{:S(2)}) collective-permute-start(bf16[4,136,1024]{2,1,0:T(8,128)(2,1)S(1)} %all_to_all.15.line), channel_id=1, source_target_pairs={{0,1},{1,0},{2,3},{3,2},{16,17},{17,16},{18,19},{19,18},{4,5},{5,4... | collective-permute-start | bytes 3342344 | tf_op jit(solution)/shard_map/ppermute | solution.py:39
  59.1 12.2 %collective-permute-start.5 = (bf16[40,1024]{1,0:T(8,128)(2,1)S(1)}, bf16[40,1024]{1,0:T(8,128)(2,1)S(1)}, u32[]{:S(2)}, u32[]{:S(2)}) collective-permute-start(bf16[40,1024]{1,0:T(8,128)(2,1)S(1)} %get-tuple-element.9.own), channel_id=1, source_target_pairs={{0,256},{1,257},{2,258},{3,259},{16,272},{17,273},{18,274},{19,275... | collective-permute-start | bytes 245768 | tf_op jit(solution)/shard_map/ppermute | solution.py:39
  71.2 2.1 %collective-permute-done.5.across = bf16[40,1024]{1,0:T(8,128)(2,1)S(1)} collective-permute-done((bf16[40,1024]{1,0:T(8,128)(2,1)S(1)}, bf16[40,1024]{1,0:T(8,128)(2,1)S(1)}, u32[]{:S(2)}, u32[]{:S(2)}) %collective-permute-start.5) | collective-permute-done | bytes 81952 | tf_op jit(solution)/shard_map/ppermute | solution.py:39
  73.4 0.6 shard_map.43.pair
  73.9 8.9 %collective-permute-start.6 = (bf16[72,1024]{1,0:T(8,128)(2,1)S(1)}, bf16[72,1024]{1,0:T(8,128)(2,1)S(1)}, u32[]{:S(2)}, u32[]{:S(2)}) collective-permute-start(bf16[72,1024]{1,0:T(8,128)(2,1)S(1)} %shard_map.43.pair), channel_id=1, source_target_pairs={{0,128},{1,385},{2,130},{3,387},{16,144},{17,401},{18,146},{19,403... | collective-permute-start | bytes 442376 | tf_op jit(solution)/shard_map/ppermute | solution.py:39
  82.8 6.1 %collective-permute-done.6.other = bf16[72,1024]{1,0:T(8,128)(2,1)S(1)} collective-permute-done((bf16[72,1024]{1,0:T(8,128)(2,1)S(1)}, bf16[72,1024]{1,0:T(8,128)(2,1)S(1)}, u32[]{:S(2)}, u32[]{:S(2)}) %collective-permute-start.6) | collective-permute-done | bytes 147488 | tf_op jit(solution)/shard_map/ppermute | solution.py:39
  88.9 0.6 shard_map.44.far
  89.5 5.0 %collective-permute-start.9 = (bf16[136,1024]{1,0:T(8,128)(2,1)S(1)}, bf16[136,1024]{1,0:T(8,128)(2,1)S(1)}, u32[]{:S(2)}, u32[]{:S(2)}) collective-permute-start(bf16[136,1024]{1,0:T(8,128)(2,1)S(1)} %shard_map.44.far), channel_id=1, source_target_pairs={{0,32},{1,33},{2,34},{3,35},{16,48},{17,49},{18,50},{19,51},{4,36}... | collective-permute-start | bytes 835592 | tf_op jit(solution)/shard_map/ppermute | solution.py:39
  94.5 5.6 %collective-permute-start.8 = (bf16[136,1024]{1,0:T(8,128)(2,1)S(1)}, bf16[136,1024]{1,0:T(8,128)(2,1)S(1)}, u32[]{:S(2)}, u32[]{:S(2)}) collective-permute-start(bf16[136,1024]{1,0:T(8,128)(2,1)S(1)} %shard_map.44.far), channel_id=1, source_target_pairs={{0,64},{1,449},{2,66},{3,451},{16,80},{17,465},{18,82},{19,467},{4... | collective-permute-start | bytes 835592 | tf_op jit(solution)/shard_map/ppermute | solution.py:39
  100.2 3.1 %collective-permute-start.7 = (bf16[136,1024]{1,0:T(8,128)(2,1)S(1)}, bf16[136,1024]{1,0:T(8,128)(2,1)S(1)}, u32[]{:S(2)}, u32[]{:S(2)}) collective-permute-start(bf16[136,1024]{1,0:T(8,128)(2,1)S(1)} %shard_map.44.far), channel_id=1, source_target_pairs={{0,480},{1,481},{2,482},{3,483},{16,496},{17,497},{18,498},{19,499... | collective-permute-start | bytes 835592 | tf_op jit(solution)/shard_map/ppermute | solution.py:39
  103.3 0.0 collective-permute-done.9.behind
  103.3 4.1 %collective-permute-done.8.across = bf16[136,1024]{1,0:T(8,128)(2,1)S(1)} collective-permute-done((bf16[136,1024]{1,0:T(8,128)(2,1)S(1)}, bf16[136,1024]{1,0:T(8,128)(2,1)S(1)}, u32[]{:S(2)}, u32[]{:S(2)}) %collective-permute-start.8) | collective-permute-done | bytes 278560 | tf_op jit(solution)/shard_map/ppermute | solution.py:39
  107.4 5.2 %collective-permute-done.7.ahead = bf16[136,1024]{1,0:T(8,128)(2,1)S(1)} collective-permute-done((bf16[136,1024]{1,0:T(8,128)(2,1)S(1)}, bf16[136,1024]{1,0:T(8,128)(2,1)S(1)}, u32[]{:S(2)}, u32[]{:S(2)}) %collective-permute-start.7) | collective-permute-done | bytes 278560 | tf_op jit(solution)/shard_map/ppermute | solution.py:39
  112.6 0.6 shard_map.45.anchors
  113.2 3.7 %shard_map.46.before = f32[4,3,8,128]{3,2,1,0:T(8,128)S(1)} custom-call(s32[4]{0:T(128)S(1)} %pad_add_fusion.at, bf16[4,136,1024]{2,1,0:T(8,128)(2,1)S(1)} %all_to_all.15.line, bf16[3,4,136,1024]{3,2,1,0:T(8,128)(2,1)S(1)} %shard_map.42.rest, bf16[520,1024]{1,0:T(8,128)(2,1)S(1)} %shard_map.45.anchors), custom_call_target="tpu_custom_call" | custom-call | tf_op jit(solution)/shard_map/pallas_call | solution.py:258
  116.9 0.0 collective-permute-done.line
  116.9 0.0 collective-permute-done.4.rest
  116.9 3.7 %shard_map.47 = f32[16,3,4,128]{3,2,1,0:T(4,128)S(1)} custom-call(s32[4]{0:T(128)S(1)} %pad_add_fusion.at, bf16[4,136,1024]{2,1,0:T(8,128)(2,1)S(1)} %collective-permute-done.line, bf16[3,4,136,1024]{3,2,1,0:T(8,128)(2,1)S(1)} %collective-permute-done.4.rest, bf16[520,1024]{1,0:T(8,128)(2,1)S(1)} %shard_map.45.anchors, f32[4,3,8,128]{3,2,1,0:T(8,128)S(1)} %shard_map.46.before), custom_call_target="tpu_custom_call" | custom-call | tf_op jit(solution)/shard_map/pallas_call | solution.py:261
  120.6 16.8 %all_to_all.16.arrived = f32[16,3,4,128]{3,2,1,0:T(4,128)S(1)} all-to-all(f32[16,3,4,128]{3,2,1,0:T(4,128)S(1)} %shard_map.47), channel_id=1, replica_groups={{0,32,64,96,128,160,192,224,256,288,320,352,384,416,448,480},{1,33,65,9..., dimensions={0} | all-to-all | bytes 196608 | tf_op jit(solution)/shard_map/all_to_all | solution.py:61
  137.4 0.7 shard_map.48
  138.1 0.5 slice_bitcast_fusion
  138.6 16.5 %all_to_all.17 = f32[32,1,128]{2,1,0:T(1,128)S(1)} all-to-all(f32[32,1,128]{2,1,0:T(1,128)S(1)} %get-tuple-element.13), channel_id=1, replica_groups={{0,1,2,3,16,17,18,19,4,5,6,7,20,21,22,23,8,9,10,11,24,25,26,27,12,13,14..., dimensions={0} | all-to-all | bytes 32768 | tf_op jit(solution)/shard_map/all_to_all | solution.py:61
  155.1 0.1 reduce_sum.11
  155.2 0.6 fusion
Async XLA Ops:
  0.8 1.0 copy-start
  1.8 0.7 copy-start.1
  18.3 18.1 %collective-permute-start.3 = (bf16[4,136,1024]{2,1,0:T(8,128)(2,1)S(1)}, bf16[4,136,1024]{2,1,0:T(8,128)(2,1)S(1)}, u32[]{:S(2)}, u32[]{:S(2)}) collective-permute-start(bf16[4,136,1024]{2,1,0:T(8,128)(2,1)S(1)} %all_to_all.15.line), channel_id=1, source_target_pairs={{0,16},{1,9},{2,18},{3,11},{16,0},{17,25},{18,2},{19,27},{4,20},{5... | collective-permute-start | bytes 3342344 | tf_op jit(solution)/shard_map/ppermute | solution.py:39
  22.7 25.7 %collective-permute-start.2 = (bf16[4,136,1024]{2,1,0:T(8,128)(2,1)S(1)}, bf16[4,136,1024]{2,1,0:T(8,128)(2,1)S(1)}, u32[]{:S(2)}, u32[]{:S(2)}) collective-permute-start(bf16[4,136,1024]{2,1,0:T(8,128)(2,1)S(1)} %all_to_all.15.line), channel_id=1, source_target_pairs={{0,18},{1,13},{2,0},{3,15},{16,2},{17,29},{18,16},{19,31},{4,22},{... | collective-permute-start | bytes 3342344 | tf_op jit(solution)/shard_map/ppermute | solution.py:39
  25.5 23.0 %collective-permute-start.1 = (bf16[4,136,1024]{2,1,0:T(8,128)(2,1)S(1)}, bf16[4,136,1024]{2,1,0:T(8,128)(2,1)S(1)}, u32[]{:S(2)}, u32[]{:S(2)}) collective-permute-start(bf16[4,136,1024]{2,1,0:T(8,128)(2,1)S(1)} %all_to_all.15.line), channel_id=1, source_target_pairs={{0,2},{1,5},{2,16},{3,7},{16,18},{17,21},{18,0},{19,23},{4,6},{5,9... | collective-permute-start | bytes 3342344 | tf_op jit(solution)/shard_map/ppermute | solution.py:39
  49.2 67.7 %collective-permute-start.4 = (bf16[3,4,136,1024]{3,2,1,0:T(8,128)(2,1)S(1)}, bf16[3,4,136,1024]{3,2,1,0:T(8,128)(2,1)S(1)}, u32[]{:S(2)}, u32[]{:S(2)}) collective-permute-start(bf16[3,4,136,1024]{3,2,1,0:T(8,128)(2,1)S(1)} %shard_map.42.rest), channel_id=1, source_target_pairs={{0,1},{1,0},{2,3},{3,2},{16,17},{17,16},{18,19},{19,18},{4,5},{5,4... | collective-permute-start | bytes 10027016 | tf_op jit(solution)/shard_map/ppermute | solution.py:39
  57.1 59.7 %collective-permute-start = (bf16[4,136,1024]{2,1,0:T(8,128)(2,1)S(1)}, bf16[4,136,1024]{2,1,0:T(8,128)(2,1)S(1)}, u32[]{:S(2)}, u32[]{:S(2)}) collective-permute-start(bf16[4,136,1024]{2,1,0:T(8,128)(2,1)S(1)} %all_to_all.15.line), channel_id=1, source_target_pairs={{0,1},{1,0},{2,3},{3,2},{16,17},{17,16},{18,19},{19,18},{4,5},{5,4... | collective-permute-start | bytes 3342344 | tf_op jit(solution)/shard_map/ppermute | solution.py:39
  59.1 14.3 %collective-permute-start.5 = (bf16[40,1024]{1,0:T(8,128)(2,1)S(1)}, bf16[40,1024]{1,0:T(8,128)(2,1)S(1)}, u32[]{:S(2)}, u32[]{:S(2)}) collective-permute-start(bf16[40,1024]{1,0:T(8,128)(2,1)S(1)} %get-tuple-element.9.own), channel_id=1, source_target_pairs={{0,256},{1,257},{2,258},{3,259},{16,272},{17,273},{18,274},{19,275... | collective-permute-start | bytes 245768 | tf_op jit(solution)/shard_map/ppermute | solution.py:39
  73.9 15.0 %collective-permute-start.6 = (bf16[72,1024]{1,0:T(8,128)(2,1)S(1)}, bf16[72,1024]{1,0:T(8,128)(2,1)S(1)}, u32[]{:S(2)}, u32[]{:S(2)}) collective-permute-start(bf16[72,1024]{1,0:T(8,128)(2,1)S(1)} %shard_map.43.pair), channel_id=1, source_target_pairs={{0,128},{1,385},{2,130},{3,387},{16,144},{17,401},{18,146},{19,403... | collective-permute-start | bytes 442376 | tf_op jit(solution)/shard_map/ppermute | solution.py:39
  89.5 13.8 %collective-permute-start.9 = (bf16[136,1024]{1,0:T(8,128)(2,1)S(1)}, bf16[136,1024]{1,0:T(8,128)(2,1)S(1)}, u32[]{:S(2)}, u32[]{:S(2)}) collective-permute-start(bf16[136,1024]{1,0:T(8,128)(2,1)S(1)} %shard_map.44.far), channel_id=1, source_target_pairs={{0,32},{1,33},{2,34},{3,35},{16,48},{17,49},{18,50},{19,51},{4,36}... | collective-permute-start | bytes 835592 | tf_op jit(solution)/shard_map/ppermute | solution.py:39
  94.5 12.9 %collective-permute-start.8 = (bf16[136,1024]{1,0:T(8,128)(2,1)S(1)}, bf16[136,1024]{1,0:T(8,128)(2,1)S(1)}, u32[]{:S(2)}, u32[]{:S(2)}) collective-permute-start(bf16[136,1024]{1,0:T(8,128)(2,1)S(1)} %shard_map.44.far), channel_id=1, source_target_pairs={{0,64},{1,449},{2,66},{3,451},{16,80},{17,465},{18,82},{19,467},{4... | collective-permute-start | bytes 835592 | tf_op jit(solution)/shard_map/ppermute | solution.py:39
  100.2 12.4 %collective-permute-start.7 = (bf16[136,1024]{1,0:T(8,128)(2,1)S(1)}, bf16[136,1024]{1,0:T(8,128)(2,1)S(1)}, u32[]{:S(2)}, u32[]{:S(2)}) collective-permute-start(bf16[136,1024]{1,0:T(8,128)(2,1)S(1)} %shard_map.44.far), channel_id=1, source_target_pairs={{0,480},{1,481},{2,482},{3,483},{16,496},{17,497},{18,498},{19,499... | collective-permute-start | bytes 835592 | tf_op jit(solution)/shard_map/ppermute | solution.py:39

commit v2 on v1

--- a/solution.py
+++ b/solution.py
@@ -209,7 +209,7 @@
     classes = lax.broadcasted_iota(jnp.int32, loss.shape, 0)
     mine = jnp.sum(jnp.where(classes == zl, loss, 0.0), axis=0, keepdims=True)
     mine = jnp.broadcast_to(mine, (8, KEYS))
-    own[...] = pltpu.roll(mine, (4 - zh) % 4 * A_DEV, 1)
+    own[...] = pltpu.roll(mine, (4 - zh) % 4 * A_DEV, 1)[0, :A_DEV]
     lane = lax.broadcasted_iota(jnp.int32, (1, KEYS), 1)
     loss_sum = jnp.sum(jnp.sum(loss, axis=0, keepdims=True), axis=1, keepdims=True)
     valid_sum = jnp.sum(
@@ -266,11 +266,11 @@
         loss_body,
         1,
         (
-            jax.ShapeDtypeStruct((8, KEYS), F32),
+            jax.ShapeDtypeStruct((A_DEV,), F32),
             jax.ShapeDtypeStruct((2 * X * Y, 1, KEYS), F32),
         ),
     )(at, arrived)
-    anchor_loss, both = lax.optimization_barrier((own_loss[0, :A_DEV], both))
+    anchor_loss, both = lax.optimization_barrier((own_loss, both))
     everyone = swapped_to_all(both, PLANES).sum(axis=0)[0]
     mean_loss = everyone[0] / jnp.maximum(everyone[1], 1.0)
     return (anchor_loss, mean_loss)

time: 159 us -> 159 us (level)
  no operation moved by 1% of the time
where the time goes in v2:
time: 159 us; the launch traced here: 158 us
  starting transfers between devices  54.3 us (34%)
  blocking collectives  48.5 us (31%)
  waiting for transfers between devices  38 us (24%)
  Pallas kernels  11.7 us (7%)
  between operations  3.33 us (2%)
  local copies, waits for them, and re-layouts  2.19 us (1%)
    ppermute x10, starting transfers between devices, moved(): lax.ppermute(block, 'd', [(device_at(*spot), device_at(*target(*spot))) f...  54.3 us
    all_to_all x3, blocking collectives, swapped_to_all(): lax.all_to_all(blocks, 'd', 0, 0, tiled=True, axis_index_groups=groups)  48.5 us
    ppermute x10, waiting for transfers between devices, moved(): lax.ppermute(block, 'd', [(device_at(*spot), device_at(*target(*spot))) f...  38 us
    pallas_call x1, Pallas kernels, loss_of(): call(theirs_body, 4, (jax.ShapeDtypeStruct((Z, 3, 4, KEYS), F32),), (), 16)  3.68 us
    pallas_call x1, Pallas kernels, loss_of(): call(mine_body, 3, (jax.ShapeDtypeStruct((4, 3, 8, KEYS), F32),), (), 16)  3.67 us
  transfers between devices with their start and end apart: 10, of which 6 were waited for; matrix products, arithmetic and copies ran while one was open for 0% of the time, Pallas kernels for 3%

profile of v2, /device:TPU:1, one launch (start us, length us, event | category | flops | bytes accessed | tf_op | source)
XLA Modules:
  0.0 158.2 jit_solution(7031226893047042055)
XLA Ops:
  0.7 0.1 pad_add_fusion.at
  0.8 0.0 copy-start
  0.8 0.9 copy-done
  1.8 0.0 copy-start.1
  1.8 0.7 copy-done.1
  2.4 0.7 shard_map.41
  3.1 15.2 %all_to_all.15.line = bf16[4,136,1024]{2,1,0:T(8,128)(2,1)S(1)} all-to-all(bf16[4,136,1024]{2,1,0:T(8,128)(2,1)S(1)} %get-tuple-element.6), channel_id=1, replica_groups={{0,4,8,12},{2,6,10,14},{16,20,24,28},{18,22,26,30},{32,36,40,44},{34,38..., dimensions={0} | all-to-all | bytes 2228224 | tf_op jit(solution)/shard_map/all_to_all | solution.py:61
  18.3 4.3 %collective-permute-start.3 = (bf16[4,136,1024]{2,1,0:T(8,128)(2,1)S(1)}, bf16[4,136,1024]{2,1,0:T(8,128)(2,1)S(1)}, u32[]{:S(2)}, u32[]{:S(2)}) collective-permute-start(bf16[4,136,1024]{2,1,0:T(8,128)(2,1)S(1)} %all_to_all.15.line), channel_id=1, source_target_pairs={{0,16},{1,9},{2,18},{3,11},{16,0},{17,25},{18,2},{19,27},{4,20},{5... | collective-permute-start | bytes 3342344 | tf_op jit(solution)/shard_map/ppermute | solution.py:39
  22.7 2.8 %collective-permute-start.2 = (bf16[4,136,1024]{2,1,0:T(8,128)(2,1)S(1)}, bf16[4,136,1024]{2,1,0:T(8,128)(2,1)S(1)}, u32[]{:S(2)}, u32[]{:S(2)}) collective-permute-start(bf16[4,136,1024]{2,1,0:T(8,128)(2,1)S(1)} %all_to_all.15.line), channel_id=1, source_target_pairs={{0,18},{1,13},{2,0},{3,15},{16,2},{17,29},{18,16},{19,31},{4,22},{... | collective-permute-start | bytes 3342344 | tf_op jit(solution)/shard_map/ppermute | solution.py:39
  25.5 2.5 %collective-permute-start.1 = (bf16[4,136,1024]{2,1,0:T(8,128)(2,1)S(1)}, bf16[4,136,1024]{2,1,0:T(8,128)(2,1)S(1)}, u32[]{:S(2)}, u32[]{:S(2)}) collective-permute-start(bf16[4,136,1024]{2,1,0:T(8,128)(2,1)S(1)} %all_to_all.15.line), channel_id=1, source_target_pairs={{0,2},{1,5},{2,16},{3,7},{16,18},{17,21},{18,0},{19,23},{4,6},{5,9... | collective-permute-start | bytes 3342344 | tf_op jit(solution)/shard_map/ppermute | solution.py:39
  28.0 8.4 %collective-permute-done.3.two = bf16[4,136,1024]{2,1,0:T(8,128)(2,1)S(1)} collective-permute-done((bf16[4,136,1024]{2,1,0:T(8,128)(2,1)S(1)}, bf16[4,136,1024]{2,1,0:T(8,128)(2,1)S(1)}, u32[]{:S(2)}, u32[]{:S(2)}) %collective-permute-start.3) | collective-permute-done | bytes 1114144 | tf_op jit(solution)/shard_map/ppermute | solution.py:39
  36.4 12.0 %collective-permute-done.2.minus = bf16[4,136,1024]{2,1,0:T(8,128)(2,1)S(1)} collective-permute-done((bf16[4,136,1024]{2,1,0:T(8,128)(2,1)S(1)}, bf16[4,136,1024]{2,1,0:T(8,128)(2,1)S(1)}, u32[]{:S(2)}, u32[]{:S(2)}) %collective-permute-start.2) | collective-permute-done | bytes 1114144 | tf_op jit(solution)/shard_map/ppermute | solution.py:39
  48.4 0.0 collective-permute-done.1.plus
  48.4 0.8 shard_map.42.rest
  49.2 7.9 %collective-permute-start.4 = (bf16[3,4,136,1024]{3,2,1,0:T(8,128)(2,1)S(1)}, bf16[3,4,136,1024]{3,2,1,0:T(8,128)(2,1)S(1)}, u32[]{:S(2)}, u32[]{:S(2)}) collective-permute-start(bf16[3,4,136,1024]{3,2,1,0:T(8,128)(2,1)S(1)} %shard_map.42.rest), channel_id=1, source_target_pairs={{0,1},{1,0},{2,3},{3,2},{16,17},{17,16},{18,19},{19,18},{4,5},{5,4... | collective-permute-start | bytes 10027016 | tf_op jit(solution)/shard_map/ppermute | solution.py:39
  57.1 1.9 %collective-permute-start = (bf16[4,136,1024]{2,1,0:T(8,128)(2,1)S(1)}, bf16[4,136,1024]{2,1,0:T(8,128)(2,1)S(1)}, u32[]{:S(2)}, u32[]{:S(2)}) collective-permute-start(bf16[4,136,1024]{2,1,0:T(8,128)(2,1)S(1)} %all_to_all.15.line), channel_id=1, source_target_pairs={{0,1},{1,0},{2,3},{3,2},{16,17},{17,16},{18,19},{19,18},{4,5},{5,4... | collective-permute-start | bytes 3342344 | tf_op jit(solution)/shard_map/ppermute | solution.py:39
  59.1 12.2 %collective-permute-start.5 = (bf16[40,1024]{1,0:T(8,128)(2,1)S(1)}, bf16[40,1024]{1,0:T(8,128)(2,1)S(1)}, u32[]{:S(2)}, u32[]{:S(2)}) collective-permute-start(bf16[40,1024]{1,0:T(8,128)(2,1)S(1)} %get-tuple-element.7.own), channel_id=1, source_target_pairs={{0,256},{1,257},{2,258},{3,259},{16,272},{17,273},{18,274},{19,275... | collective-permute-start | bytes 245768 | tf_op jit(solution)/shard_map/ppermute | solution.py:39
  71.2 2.1 %collective-permute-done.5.across = bf16[40,1024]{1,0:T(8,128)(2,1)S(1)} collective-permute-done((bf16[40,1024]{1,0:T(8,128)(2,1)S(1)}, bf16[40,1024]{1,0:T(8,128)(2,1)S(1)}, u32[]{:S(2)}, u32[]{:S(2)}) %collective-permute-start.5) | collective-permute-done | bytes 81952 | tf_op jit(solution)/shard_map/ppermute | solution.py:39
  73.4 0.6 shard_map.43.pair
  73.9 8.9 %collective-permute-start.6 = (bf16[72,1024]{1,0:T(8,128)(2,1)S(1)}, bf16[72,1024]{1,0:T(8,128)(2,1)S(1)}, u32[]{:S(2)}, u32[]{:S(2)}) collective-permute-start(bf16[72,1024]{1,0:T(8,128)(2,1)S(1)} %shard_map.43.pair), channel_id=1, source_target_pairs={{0,128},{1,385},{2,130},{3,387},{16,144},{17,401},{18,146},{19,403... | collective-permute-start | bytes 442376 | tf_op jit(solution)/shard_map/ppermute | solution.py:39
  82.8 6.1 %collective-permute-done.6.other = bf16[72,1024]{1,0:T(8,128)(2,1)S(1)} collective-permute-done((bf16[72,1024]{1,0:T(8,128)(2,1)S(1)}, bf16[72,1024]{1,0:T(8,128)(2,1)S(1)}, u32[]{:S(2)}, u32[]{:S(2)}) %collective-permute-start.6) | collective-permute-done | bytes 147488 | tf_op jit(solution)/shard_map/ppermute | solution.py:39
  88.9 0.6 shard_map.44.far
  89.5 5.0 %collective-permute-start.9 = (bf16[136,1024]{1,0:T(8,128)(2,1)S(1)}, bf16[136,1024]{1,0:T(8,128)(2,1)S(1)}, u32[]{:S(2)}, u32[]{:S(2)}) collective-permute-start(bf16[136,1024]{1,0:T(8,128)(2,1)S(1)} %shard_map.44.far), channel_id=1, source_target_pairs={{0,32},{1,33},{2,34},{3,35},{16,48},{17,49},{18,50},{19,51},{4,36}... | collective-permute-start | bytes 835592 | tf_op jit(solution)/shard_map/ppermute | solution.py:39
  94.5 5.6 %collective-permute-start.8 = (bf16[136,1024]{1,0:T(8,128)(2,1)S(1)}, bf16[136,1024]{1,0:T(8,128)(2,1)S(1)}, u32[]{:S(2)}, u32[]{:S(2)}) collective-permute-start(bf16[136,1024]{1,0:T(8,128)(2,1)S(1)} %shard_map.44.far), channel_id=1, source_target_pairs={{0,64},{1,449},{2,66},{3,451},{16,80},{17,465},{18,82},{19,467},{4... | collective-permute-start | bytes 835592 | tf_op jit(solution)/shard_map/ppermute | solution.py:39
  100.2 3.1 %collective-permute-start.7 = (bf16[136,1024]{1,0:T(8,128)(2,1)S(1)}, bf16[136,1024]{1,0:T(8,128)(2,1)S(1)}, u32[]{:S(2)}, u32[]{:S(2)}) collective-permute-start(bf16[136,1024]{1,0:T(8,128)(2,1)S(1)} %shard_map.44.far), channel_id=1, source_target_pairs={{0,480},{1,481},{2,482},{3,483},{16,496},{17,497},{18,498},{19,499... | collective-permute-start | bytes 835592 | tf_op jit(solution)/shard_map/ppermute | solution.py:39
  103.3 0.0 collective-permute-done.9.behind
  103.3 4.1 %collective-permute-done.8.across = bf16[136,1024]{1,0:T(8,128)(2,1)S(1)} collective-permute-done((bf16[136,1024]{1,0:T(8,128)(2,1)S(1)}, bf16[136,1024]{1,0:T(8,128)(2,1)S(1)}, u32[]{:S(2)}, u32[]{:S(2)}) %collective-permute-start.8) | collective-permute-done | bytes 278560 | tf_op jit(solution)/shard_map/ppermute | solution.py:39
  107.4 5.2 %collective-permute-done.7.ahead = bf16[136,1024]{1,0:T(8,128)(2,1)S(1)} collective-permute-done((bf16[136,1024]{1,0:T(8,128)(2,1)S(1)}, bf16[136,1024]{1,0:T(8,128)(2,1)S(1)}, u32[]{:S(2)}, u32[]{:S(2)}) %collective-permute-start.7) | collective-permute-done | bytes 278560 | tf_op jit(solution)/shard_map/ppermute | solution.py:39
  112.6 0.6 shard_map.45.anchors
  113.2 3.7 %shard_map.46.before = f32[4,3,8,128]{3,2,1,0:T(8,128)S(1)} custom-call(s32[4]{0:T(128)S(1)} %pad_add_fusion.at, bf16[4,136,1024]{2,1,0:T(8,128)(2,1)S(1)} %all_to_all.15.line, bf16[3,4,136,1024]{3,2,1,0:T(8,128)(2,1)S(1)} %shard_map.42.rest, bf16[520,1024]{1,0:T(8,128)(2,1)S(1)} %shard_map.45.anchors), custom_call_target="tpu_custom_call" | custom-call | tf_op jit(solution)/shard_map/pallas_call | solution.py:258
  116.9 0.0 collective-permute-done.line
  116.9 0.0 collective-permute-done.4.rest
  116.9 3.7 %shard_map.47 = f32[16,3,4,128]{3,2,1,0:T(4,128)S(1)} custom-call(s32[4]{0:T(128)S(1)} %pad_add_fusion.at, bf16[4,136,1024]{2,1,0:T(8,128)(2,1)S(1)} %collective-permute-done.line, bf16[3,4,136,1024]{3,2,1,0:T(8,128)(2,1)S(1)} %collective-permute-done.4.rest, bf16[520,1024]{1,0:T(8,128)(2,1)S(1)} %shard_map.45.anchors, f32[4,3,8,128]{3,2,1,0:T(8,128)S(1)} %shard_map.46.before), custom_call_target="tpu_custom_call" | custom-call | tf_op jit(solution)/shard_map/pallas_call | solution.py:261
  120.6 16.8 %all_to_all.16.arrived = f32[16,3,4,128]{3,2,1,0:T(4,128)S(1)} all-to-all(f32[16,3,4,128]{3,2,1,0:T(4,128)S(1)} %shard_map.47), channel_id=1, replica_groups={{0,32,64,96,128,160,192,224,256,288,320,352,384,416,448,480},{1,33,65,9..., dimensions={0} | all-to-all | bytes 196608 | tf_op jit(solution)/shard_map/all_to_all | solution.py:61
  137.4 1.2 shard_map.48
  138.6 16.5 %all_to_all.17 = f32[32,1,128]{2,1,0:T(1,128)S(1)} all-to-all(f32[32,1,128]{2,1,0:T(1,128)S(1)} %get-tuple-element.9), channel_id=1, replica_groups={{0,1,2,3,16,17,18,19,4,5,6,7,20,21,22,23,8,9,10,11,24,25,26,27,12,13,14..., dimensions={0} | all-to-all | bytes 32768 | tf_op jit(solution)/shard_map/all_to_all | solution.py:61
  155.1 0.1 reduce_sum.11
  155.2 0.6 fusion
Async XLA Ops:
  0.8 1.0 copy-start
  1.8 0.7 copy-start.1
  18.3 18.1 %collective-permute-start.3 = (bf16[4,136,1024]{2,1,0:T(8,128)(2,1)S(1)}, bf16[4,136,1024]{2,1,0:T(8,128)(2,1)S(1)}, u32[]{:S(2)}, u32[]{:S(2)}) collective-permute-start(bf16[4,136,1024]{2,1,0:T(8,128)(2,1)S(1)} %all_to_all.15.line), channel_id=1, source_target_pairs={{0,16},{1,9},{2,18},{3,11},{16,0},{17,25},{18,2},{19,27},{4,20},{5... | collective-permute-start | bytes 3342344 | tf_op jit(solution)/shard_map/ppermute | solution.py:39
  22.7 25.7 %collective-permute-start.2 = (bf16[4,136,1024]{2,1,0:T(8,128)(2,1)S(1)}, bf16[4,136,1024]{2,1,0:T(8,128)(2,1)S(1)}, u32[]{:S(2)}, u32[]{:S(2)}) collective-permute-start(bf16[4,136,1024]{2,1,0:T(8,128)(2,1)S(1)} %all_to_all.15.line), channel_id=1, source_target_pairs={{0,18},{1,13},{2,0},{3,15},{16,2},{17,29},{18,16},{19,31},{4,22},{... | collective-permute-start | bytes 3342344 | tf_op jit(solution)/shard_map/ppermute | solution.py:39
  25.5 23.0 %collective-permute-start.1 = (bf16[4,136,1024]{2,1,0:T(8,128)(2,1)S(1)}, bf16[4,136,1024]{2,1,0:T(8,128)(2,1)S(1)}, u32[]{:S(2)}, u32[]{:S(2)}) collective-permute-start(bf16[4,136,1024]{2,1,0:T(8,128)(2,1)S(1)} %all_to_all.15.line), channel_id=1, source_target_pairs={{0,2},{1,5},{2,16},{3,7},{16,18},{17,21},{18,0},{19,23},{4,6},{5,9... | collective-permute-start | bytes 3342344 | tf_op jit(solution)/shard_map/ppermute | solution.py:39
  49.2 67.7 %collective-permute-start.4 = (bf16[3,4,136,1024]{3,2,1,0:T(8,128)(2,1)S(1)}, bf16[3,4,136,1024]{3,2,1,0:T(8,128)(2,1)S(1)}, u32[]{:S(2)}, u32[]{:S(2)}) collective-permute-start(bf16[3,4,136,1024]{3,2,1,0:T(8,128)(2,1)S(1)} %shard_map.42.rest), channel_id=1, source_target_pairs={{0,1},{1,0},{2,3},{3,2},{16,17},{17,16},{18,19},{19,18},{4,5},{5,4... | collective-permute-start | bytes 10027016 | tf_op jit(solution)/shard_map/ppermute | solution.py:39
  57.1 59.8 %collective-permute-start = (bf16[4,136,1024]{2,1,0:T(8,128)(2,1)S(1)}, bf16[4,136,1024]{2,1,0:T(8,128)(2,1)S(1)}, u32[]{:S(2)}, u32[]{:S(2)}) collective-permute-start(bf16[4,136,1024]{2,1,0:T(8,128)(2,1)S(1)} %all_to_all.15.line), channel_id=1, source_target_pairs={{0,1},{1,0},{2,3},{3,2},{16,17},{17,16},{18,19},{19,18},{4,5},{5,4... | collective-permute-start | bytes 3342344 | tf_op jit(solution)/shard_map/ppermute | solution.py:39
  59.1 14.3 %collective-permute-start.5 = (bf16[40,1024]{1,0:T(8,128)(2,1)S(1)}, bf16[40,1024]{1,0:T(8,128)(2,1)S(1)}, u32[]{:S(2)}, u32[]{:S(2)}) collective-permute-start(bf16[40,1024]{1,0:T(8,128)(2,1)S(1)} %get-tuple-element.7.own), channel_id=1, source_target_pairs={{0,256},{1,257},{2,258},{3,259},{16,272},{17,273},{18,274},{19,275... | collective-permute-start | bytes 245768 | tf_op jit(solution)/shard_map/ppermute | solution.py:39
  73.9 15.0 %collective-permute-start.6 = (bf16[72,1024]{1,0:T(8,128)(2,1)S(1)}, bf16[72,1024]{1,0:T(8,128)(2,1)S(1)}, u32[]{:S(2)}, u32[]{:S(2)}) collective-permute-start(bf16[72,1024]{1,0:T(8,128)(2,1)S(1)} %shard_map.43.pair), channel_id=1, source_target_pairs={{0,128},{1,385},{2,130},{3,387},{16,144},{17,401},{18,146},{19,403... | collective-permute-start | bytes 442376 | tf_op jit(solution)/shard_map/ppermute | solution.py:39
  89.5 13.8 %collective-permute-start.9 = (bf16[136,1024]{1,0:T(8,128)(2,1)S(1)}, bf16[136,1024]{1,0:T(8,128)(2,1)S(1)}, u32[]{:S(2)}, u32[]{:S(2)}) collective-permute-start(bf16[136,1024]{1,0:T(8,128)(2,1)S(1)} %shard_map.44.far), channel_id=1, source_target_pairs={{0,32},{1,33},{2,34},{3,35},{16,48},{17,49},{18,50},{19,51},{4,36}... | collective-permute-start | bytes 835592 | tf_op jit(solution)/shard_map/ppermute | solution.py:39
  94.5 12.9 %collective-permute-start.8 = (bf16[136,1024]{1,0:T(8,128)(2,1)S(1)}, bf16[136,1024]{1,0:T(8,128)(2,1)S(1)}, u32[]{:S(2)}, u32[]{:S(2)}) collective-permute-start(bf16[136,1024]{1,0:T(8,128)(2,1)S(1)} %shard_map.44.far), channel_id=1, source_target_pairs={{0,64},{1,449},{2,66},{3,451},{16,80},{17,465},{18,82},{19,467},{4... | collective-permute-start | bytes 835592 | tf_op jit(solution)/shard_map/ppermute | solution.py:39
  100.2 12.4 %collective-permute-start.7 = (bf16[136,1024]{1,0:T(8,128)(2,1)S(1)}, bf16[136,1024]{1,0:T(8,128)(2,1)S(1)}, u32[]{:S(2)}, u32[]{:S(2)}) collective-permute-start(bf16[136,1024]{1,0:T(8,128)(2,1)S(1)} %shard_map.44.far), channel_id=1, source_target_pairs={{0,480},{1,481},{2,482},{3,483},{16,496},{17,497},{18,498},{19,499... | collective-permute-start | bytes 835592 | tf_op jit(solution)/shard_map/ppermute | solution.py:39

commit v3 on v2

--- a/solution.py
+++ b/solution.py
@@ -104,26 +104,20 @@
         anchors[A_DEV:, k * KEYS : (k + 1) * KEYS] = mine.astype(BF16)
 
 
-def pair_body(at, own, across, pair):
-    pair[:A_DEV, :] = own[:A_DEV, :]
-    pair[A_DEV : 2 * A_DEV, :] = across[:A_DEV, :]
-    tail = own[A_DEV:, :].astype(F32) + across[A_DEV:, :].astype(F32)
-    pair[2 * A_DEV :, :] = tail.astype(BF16)
-
-
-def far_body(at, pair, other, far):
-    zh, c = at[0], at[3]
-    for step, ref, k in ((0, pair, 0), (2, pair, 1), (3 + 2 * c, other, 0), (1 + 2 * c, other, 1)):
+def far_body(at, own, before, after, across, far):
+    zh = at[0]
+    tail = None
+    for step, ref in ((0, own), (3, before), (1, after), (2, across)):
         slot = (zh + step) % 4
-        block = ref[k * A_DEV : (k + 1) * A_DEV, :]
-        far[pl.ds(pl.multiple_of(slot * A_DEV, A_DEV), A_DEV), :] = block
-    tail = pair[2 * A_DEV :, :].astype(F32) + other[2 * A_DEV :, :].astype(F32)
+        far[pl.ds(pl.multiple_of(slot * A_DEV, A_DEV), A_DEV), :] = ref[:A_DEV, :]
+        label = ref[A_DEV:, :].astype(F32)
+        tail = label if tail is None else tail + label
     far[KEYS:, :] = tail.astype(BF16)
 
 
-def rest_body(at, plus, minus, two, rest):
-    for k, ref in enumerate((plus, minus, two)):
-        rest[k] = ref[...]
+def keys_body(at, line, plus, minus, two, keys):
+    for k, ref in enumerate((line, plus, minus, two)):
+        keys[k] = ref[...]
 
 
 def anchors_body(at, far, ahead, across, behind, anchors):
@@ -177,17 +171,17 @@
                     totals[d][m] += part.reshape(n // 8, 8, n).sum(axis=0)
 
 
-def mine_body(at, line, rest, anchors, out):
+def mine_body(at, keys, anchors, out):
     totals = [[jnp.zeros((8, KEYS), F32) for _ in range(3)] for _ in range(4)]
-    scores_of(at, (line, rest.at[0], rest.at[1], rest.at[2]), anchors, totals, True)
+    scores_of(at, [keys.at[p] for p in range(4)], anchors, totals, True)
     for d in range(4):
         for k in range(3):
             out[d, k] = totals[d][k]
 
 
-def theirs_body(at, line, rest, anchors, before, out):
+def theirs_body(at, keys, anchors, before, out):
     totals = [[before[d, k] for k in range(3)] for d in range(4)]
-    scores_of(at, (line, rest.at[0], rest.at[1], rest.at[2]), anchors, totals, False)
+    scores_of(at, [keys.at[p] for p in range(4)], anchors, totals, False)
     for d in range(4):
         slot = (at[1] + d) % 4
         for k in range(3):
@@ -237,30 +231,31 @@
     line = swapped_to_all(own_keys, LINES)
     across = along_z(own_anchors, 8)
 
+    before = along_z(own_anchors, 4)
+    after = along_z(own_anchors, -4)
+
     plane = []
     for step in (1, -1, 2):
         plane.append(across_lines(line, step))
 
-    two = jax.ShapeDtypeStruct((2 * A_DEV + LAB, D), BF16)
-    (pair,) = call(pair_body, 2, (two,))(at, own_anchors, across)
-    other_pair = split_along_z(pair, 4)
-    (far,) = call(far_body, 2, (jax.ShapeDtypeStruct((ROWS, D), BF16),))(at, pair, other_pair)
+    (far,) = call(far_body, 4, (jax.ShapeDtypeStruct((ROWS, D), BF16),))(
+        at, own_anchors, before, after, across
+    )
     across_near = split_along_z(far, 2)
     behind = along_z(far, 1)
     ahead = along_z(far, -1)
 
-    (rest,) = call(rest_body, 3, (jax.ShapeDtypeStruct((3, 4, ROWS, D), BF16),))(at, *plane)
-    other_line = other_core(line)
-    other_rest = other_core(rest)
+    (keys,) = call(keys_body, 4, (jax.ShapeDtypeStruct((4, 4, ROWS, D), BF16),))(at, line, *plane)
+    other_keys = other_core(keys)
 
     column = jax.ShapeDtypeStruct((4 * KEYS + LAB, D), BF16)
     (anchors,) = call(anchors_body, 4, (column,))(at, far, ahead, across_near, behind)
-    (first,) = call(mine_body, 3, (jax.ShapeDtypeStruct((4, 3, 8, KEYS), F32),), (), 16)(
-        at, line, rest, anchors
+    (first,) = call(mine_body, 2, (jax.ShapeDtypeStruct((4, 3, 8, KEYS), F32),), (), 16)(
+        at, keys, anchors
     )
     (sums,) = call(
-        theirs_body, 4, (jax.ShapeDtypeStruct((Z, 3, 4, KEYS), F32),), (), 16
-    )(at, other_line, other_rest, anchors, first)
+        theirs_body, 3, (jax.ShapeDtypeStruct((Z, 3, 4, KEYS), F32),), (), 16
+    )(at, other_keys, anchors, first)
     arrived = swapped_to_all(sums, COLUMNS)
     own_loss, both = call(
         loss_body,

time: 159 us -> 153 us (0.962)
  starting transfers between devices: 54.3 us -> 48.5 us
    ppermute x10, starting transfers between devices: 54.3 us -> 48.5 us  [moved(): lax.ppermute(block, 'd', [(device_at(*spot), device_at(*target(*spot))) f...]
    pallas_call x5 -> x4, Pallas kernels: 9.24 us -> 8.77 us  [the longest x1 3.7 us: loss_of(): call(theirs_body, 3, (jax.ShapeDtypeStruct((Z, 3, 4, KEYS), F32),), (), 16)]
where the time goes in v3:
time: 153 us; the launch traced here: 152 us
  blocking collectives  48.9 us (32%)
  starting transfers between devices  48.5 us (32%)
  waiting for transfers between devices  38 us (25%)
  Pallas kernels  11.2 us (7%)
  between operations  3.31 us (2%)
  local copies, waits for them, and re-layouts  2.19 us (1%)
    all_to_all x3, blocking collectives, swapped_to_all(): lax.all_to_all(blocks, 'd', 0, 0, tiled=True, axis_index_groups=groups)  48.9 us
    ppermute x10, starting transfers between devices, moved(): lax.ppermute(block, 'd', [(device_at(*spot), device_at(*target(*spot))) f...  48.5 us
    ppermute x10, waiting for transfers between devices, moved(): lax.ppermute(block, 'd', [(device_at(*spot), device_at(*target(*spot))) f...  38 us
    pallas_call x1, Pallas kernels, loss_of(): call(theirs_body, 3, (jax.ShapeDtypeStruct((Z, 3, 4, KEYS), F32),), (), 16)  3.7 us
    pallas_call x1, Pallas kernels, loss_of(): call(mine_body, 2, (jax.ShapeDtypeStruct((4, 3, 8, KEYS), F32),), (), 16)  3.67 us
  transfers between devices with their start and end apart: 10, of which 6 were waited for; matrix products, arithmetic and copies ran while one was open for 0% of the time, Pallas kernels for 3%

profile of v3, /device:TPU:1, one launch (start us, length us, event | category | flops | bytes accessed | tf_op | source)
XLA Modules:
  0.0 152.4 jit_solution(7219233724601207779)
XLA Ops:
  0.7 0.1 pad_add_fusion.at
  0.8 0.0 copy-start
  0.8 0.9 copy-done
  1.8 0.0 copy-start.1
  1.8 0.7 copy-done.1
  2.4 0.7 shard_map.41
  3.1 15.2 %all_to_all.15.line = bf16[4,136,1024]{2,1,0:T(8,128)(2,1)S(1)} all-to-all(bf16[4,136,1024]{2,1,0:T(8,128)(2,1)S(1)} %get-tuple-element.6), channel_id=1, replica_groups={{0,4,8,12},{2,6,10,14},{16,20,24,28},{18,22,26,30},{32,36,40,44},{34,38..., dimensions={0} | all-to-all | bytes 2228224 | tf_op jit(solution)/shard_map/all_to_all | solution.py:61
  18.3 4.3 %collective-permute-start.2 = (bf16[4,136,1024]{2,1,0:T(8,128)(2,1)S(1)}, bf16[4,136,1024]{2,1,0:T(8,128)(2,1)S(1)}, u32[]{:S(2)}, u32[]{:S(2)}) collective-permute-start(bf16[4,136,1024]{2,1,0:T(8,128)(2,1)S(1)} %all_to_all.15.line), channel_id=1, source_target_pairs={{0,16},{1,9},{2,18},{3,11},{16,0},{17,25},{18,2},{19,27},{4,20},{5... | collective-permute-start | bytes 3342344 | tf_op jit(solution)/shard_map/ppermute | solution.py:39
  22.7 2.8 %collective-permute-start.1 = (bf16[4,136,1024]{2,1,0:T(8,128)(2,1)S(1)}, bf16[4,136,1024]{2,1,0:T(8,128)(2,1)S(1)}, u32[]{:S(2)}, u32[]{:S(2)}) collective-permute-start(bf16[4,136,1024]{2,1,0:T(8,128)(2,1)S(1)} %all_to_all.15.line), channel_id=1, source_target_pairs={{0,18},{1,13},{2,0},{3,15},{16,2},{17,29},{18,16},{19,31},{4,22},{... | collective-permute-start | bytes 3342344 | tf_op jit(solution)/shard_map/ppermute | solution.py:39
  25.5 2.5 %collective-permute-start = (bf16[4,136,1024]{2,1,0:T(8,128)(2,1)S(1)}, bf16[4,136,1024]{2,1,0:T(8,128)(2,1)S(1)}, u32[]{:S(2)}, u32[]{:S(2)}) collective-permute-start(bf16[4,136,1024]{2,1,0:T(8,128)(2,1)S(1)} %all_to_all.15.line), channel_id=1, source_target_pairs={{0,2},{1,5},{2,16},{3,7},{16,18},{17,21},{18,0},{19,23},{4,6},{5,9... | collective-permute-start | bytes 3342344 | tf_op jit(solution)/shard_map/ppermute | solution.py:39
  28.0 8.4 %collective-permute-done.2.two = bf16[4,136,1024]{2,1,0:T(8,128)(2,1)S(1)} collective-permute-done((bf16[4,136,1024]{2,1,0:T(8,128)(2,1)S(1)}, bf16[4,136,1024]{2,1,0:T(8,128)(2,1)S(1)}, u32[]{:S(2)}, u32[]{:S(2)}) %collective-permute-start.2) | collective-permute-done | bytes 1114144 | tf_op jit(solution)/shard_map/ppermute | solution.py:39
  36.4 12.0 %collective-permute-done.1.minus = bf16[4,136,1024]{2,1,0:T(8,128)(2,1)S(1)} collective-permute-done((bf16[4,136,1024]{2,1,0:T(8,128)(2,1)S(1)}, bf16[4,136,1024]{2,1,0:T(8,128)(2,1)S(1)}, u32[]{:S(2)}, u32[]{:S(2)}) %collective-permute-start.1) | collective-permute-done | bytes 1114144 | tf_op jit(solution)/shard_map/ppermute | solution.py:39
  48.4 0.0 collective-permute-done.plus
  48.4 0.8 shard_map.42.keys
  49.3 7.9 %collective-permute-start.3 = (bf16[4,4,136,1024]{3,2,1,0:T(8,128)(2,1)S(1)}, bf16[4,4,136,1024]{3,2,1,0:T(8,128)(2,1)S(1)}, u32[]{:S(2)}, u32[]{:S(2)}) collective-permute-start(bf16[4,4,136,1024]{3,2,1,0:T(8,128)(2,1)S(1)} %shard_map.42.keys), channel_id=1, source_target_pairs={{0,1},{1,0},{2,3},{3,2},{16,17},{17,16},{18,19},{19,18},{4,5},{5,4... | collective-permute-start | bytes 13369352 | tf_op jit(solution)/shard_map/ppermute | solution.py:39
  57.2 12.2 %collective-permute-start.6 = (bf16[40,1024]{1,0:T(8,128)(2,1)S(1)}, bf16[40,1024]{1,0:T(8,128)(2,1)S(1)}, u32[]{:S(2)}, u32[]{:S(2)}) collective-permute-start(bf16[40,1024]{1,0:T(8,128)(2,1)S(1)} %get-tuple-element.7.own), channel_id=1, source_target_pairs={{0,256},{1,257},{2,258},{3,259},{16,272},{17,273},{18,274},{19,275... | collective-permute-start | bytes 245768 | tf_op jit(solution)/shard_map/ppermute | solution.py:39
  69.4 1.9 %collective-permute-start.5 = (bf16[40,1024]{1,0:T(8,128)(2,1)S(1)}, bf16[40,1024]{1,0:T(8,128)(2,1)S(1)}, u32[]{:S(2)}, u32[]{:S(2)}) collective-permute-start(bf16[40,1024]{1,0:T(8,128)(2,1)S(1)} %get-tuple-element.7.own), channel_id=1, source_target_pairs={{0,384},{1,385},{2,386},{3,387},{16,400},{17,401},{18,402},{19,403... | collective-permute-start | bytes 245768 | tf_op jit(solution)/shard_map/ppermute | solution.py:39
  71.3 7.3 %collective-permute-start.4 = (bf16[40,1024]{1,0:T(8,128)(2,1)S(1)}, bf16[40,1024]{1,0:T(8,128)(2,1)S(1)}, u32[]{:S(2)}, u32[]{:S(2)}) collective-permute-start(bf16[40,1024]{1,0:T(8,128)(2,1)S(1)} %get-tuple-element.7.own), channel_id=1, source_target_pairs={{0,128},{1,129},{2,130},{3,131},{16,144},{17,145},{18,146},{19,147... | collective-permute-start | bytes 245768 | tf_op jit(solution)/shard_map/ppermute | solution.py:39
  78.6 0.0 collective-permute-done.6.across
  78.6 6.5 %collective-permute-done.5.after = bf16[40,1024]{1,0:T(8,128)(2,1)S(1)} collective-permute-done((bf16[40,1024]{1,0:T(8,128)(2,1)S(1)}, bf16[40,1024]{1,0:T(8,128)(2,1)S(1)}, u32[]{:S(2)}, u32[]{:S(2)}) %collective-permute-start.5) | collective-permute-done | bytes 81952 | tf_op jit(solution)/shard_map/ppermute | solution.py:39
  85.1 0.0 collective-permute-done.4.before
  85.1 0.6 shard_map.43.far
  85.7 3.2 %collective-permute-start.9 = (bf16[136,1024]{1,0:T(8,128)(2,1)S(1)}, bf16[136,1024]{1,0:T(8,128)(2,1)S(1)}, u32[]{:S(2)}, u32[]{:S(2)}) collective-permute-start(bf16[136,1024]{1,0:T(8,128)(2,1)S(1)} %shard_map.43.far), channel_id=1, source_target_pairs={{0,32},{1,33},{2,34},{3,35},{16,48},{17,49},{18,50},{19,51},{4,36}... | collective-permute-start | bytes 835592 | tf_op jit(solution)/shard_map/ppermute | solution.py:39
  88.9 4.5 %collective-permute-start.8 = (bf16[136,1024]{1,0:T(8,128)(2,1)S(1)}, bf16[136,1024]{1,0:T(8,128)(2,1)S(1)}, u32[]{:S(2)}, u32[]{:S(2)}) collective-permute-start(bf16[136,1024]{1,0:T(8,128)(2,1)S(1)} %shard_map.43.far), channel_id=1, source_target_pairs={{0,64},{1,449},{2,66},{3,451},{16,80},{17,465},{18,82},{19,467},{4... | collective-permute-start | bytes 835592 | tf_op jit(solution)/shard_map/ppermute | solution.py:39
  93.4 1.9 %collective-permute-start.7 = (bf16[136,1024]{1,0:T(8,128)(2,1)S(1)}, bf16[136,1024]{1,0:T(8,128)(2,1)S(1)}, u32[]{:S(2)}, u32[]{:S(2)}) collective-permute-start(bf16[136,1024]{1,0:T(8,128)(2,1)S(1)} %shard_map.43.far), channel_id=1, source_target_pairs={{0,480},{1,481},{2,482},{3,483},{16,496},{17,497},{18,498},{19,499... | collective-permute-start | bytes 835592 | tf_op jit(solution)/shard_map/ppermute | solution.py:39
  95.3 1.0 collective-permute-done.9.behind
  96.3 5.4 %collective-permute-done.8.across = bf16[136,1024]{1,0:T(8,128)(2,1)S(1)} collective-permute-done((bf16[136,1024]{1,0:T(8,128)(2,1)S(1)}, bf16[136,1024]{1,0:T(8,128)(2,1)S(1)}, u32[]{:S(2)}, u32[]{:S(2)}) %collective-permute-start.8) | collective-permute-done | bytes 278560 | tf_op jit(solution)/shard_map/ppermute | solution.py:39
  101.7 4.7 %collective-permute-done.7.ahead = bf16[136,1024]{1,0:T(8,128)(2,1)S(1)} collective-permute-done((bf16[136,1024]{1,0:T(8,128)(2,1)S(1)}, bf16[136,1024]{1,0:T(8,128)(2,1)S(1)}, u32[]{:S(2)}, u32[]{:S(2)}) %collective-permute-start.7) | collective-permute-done | bytes 278560 | tf_op jit(solution)/shard_map/ppermute | solution.py:39
  106.4 0.6 shard_map.44.anchors
  107.0 3.7 %shard_map.45.before = f32[4,3,8,128]{3,2,1,0:T(8,128)S(1)} custom-call(s32[4]{0:T(128)S(1)} %pad_add_fusion.at, bf16[4,4,136,1024]{3,2,1,0:T(8,128)(2,1)S(1)} %shard_map.42.keys, bf16[520,1024]{1,0:T(8,128)(2,1)S(1)} %shard_map.44.anchors), custom_call_target="tpu_custom_call" | custom-call | tf_op jit(solution)/shard_map/pallas_call | solution.py:253
  110.7 0.0 collective-permute-done.3.keys
  110.7 3.7 %shard_map.46 = f32[16,3,4,128]{3,2,1,0:T(4,128)S(1)} custom-call(s32[4]{0:T(128)S(1)} %pad_add_fusion.at, bf16[4,4,136,1024]{3,2,1,0:T(8,128)(2,1)S(1)} %collective-permute-done.3.keys, bf16[520,1024]{1,0:T(8,128)(2,1)S(1)} %shard_map.44.anchors, f32[4,3,8,128]{3,2,1,0:T(8,128)S(1)} %shard_map.45.before), custom_call_target="tpu_custom_call" | custom-call | tf_op jit(solution)/shard_map/pallas_call | solution.py:256
  114.4 19.7 %all_to_all.16.arrived = f32[16,3,4,128]{3,2,1,0:T(4,128)S(1)} all-to-all(f32[16,3,4,128]{3,2,1,0:T(4,128)S(1)} %shard_map.46), channel_id=1, replica_groups={{0,32,64,96,128,160,192,224,256,288,320,352,384,416,448,480},{1,33,65,9..., dimensions={0} | all-to-all | bytes 196608 | tf_op jit(solution)/shard_map/all_to_all | solution.py:61
  134.1 1.2 shard_map.47
  135.2 14.1 %all_to_all.17 = f32[32,1,128]{2,1,0:T(1,128)S(1)} all-to-all(f32[32,1,128]{2,1,0:T(1,128)S(1)} %get-tuple-element.9), channel_id=1, replica_groups={{0,1,2,3,16,17,18,19,4,5,6,7,20,21,22,23,8,9,10,11,24,25,26,27,12,13,14..., dimensions={0} | all-to-all | bytes 32768 | tf_op jit(solution)/shard_map/all_to_all | solution.py:61
  149.3 0.1 reduce_sum.11
  149.4 0.6 fusion
Async XLA Ops:
  0.8 1.0 copy-start
  1.8 0.7 copy-start.1
  18.3 18.1 %collective-permute-start.2 = (bf16[4,136,1024]{2,1,0:T(8,128)(2,1)S(1)}, bf16[4,136,1024]{2,1,0:T(8,128)(2,1)S(1)}, u32[]{:S(2)}, u32[]{:S(2)}) collective-permute-start(bf16[4,136,1024]{2,1,0:T(8,128)(2,1)S(1)} %all_to_all.15.line), channel_id=1, source_target_pairs={{0,16},{1,9},{2,18},{3,11},{16,0},{17,25},{18,2},{19,27},{4,20},{5... | collective-permute-start | bytes 3342344 | tf_op jit(solution)/shard_map/ppermute | solution.py:39
  22.7 25.7 %collective-permute-start.1 = (bf16[4,136,1024]{2,1,0:T(8,128)(2,1)S(1)}, bf16[4,136,1024]{2,1,0:T(8,128)(2,1)S(1)}, u32[]{:S(2)}, u32[]{:S(2)}) collective-permute-start(bf16[4,136,1024]{2,1,0:T(8,128)(2,1)S(1)} %all_to_all.15.line), channel_id=1, source_target_pairs={{0,18},{1,13},{2,0},{3,15},{16,2},{17,29},{18,16},{19,31},{4,22},{... | collective-permute-start | bytes 3342344 | tf_op jit(solution)/shard_map/ppermute | solution.py:39
  25.5 23.0 %collective-permute-start = (bf16[4,136,1024]{2,1,0:T(8,128)(2,1)S(1)}, bf16[4,136,1024]{2,1,0:T(8,128)(2,1)S(1)}, u32[]{:S(2)}, u32[]{:S(2)}) collective-permute-start(bf16[4,136,1024]{2,1,0:T(8,128)(2,1)S(1)} %all_to_all.15.line), channel_id=1, source_target_pairs={{0,2},{1,5},{2,16},{3,7},{16,18},{17,21},{18,0},{19,23},{4,6},{5,9... | collective-permute-start | bytes 3342344 | tf_op jit(solution)/shard_map/ppermute | solution.py:39
  49.3 61.4 %collective-permute-start.3 = (bf16[4,4,136,1024]{3,2,1,0:T(8,128)(2,1)S(1)}, bf16[4,4,136,1024]{3,2,1,0:T(8,128)(2,1)S(1)}, u32[]{:S(2)}, u32[]{:S(2)}) collective-permute-start(bf16[4,4,136,1024]{3,2,1,0:T(8,128)(2,1)S(1)} %shard_map.42.keys), channel_id=1, source_target_pairs={{0,1},{1,0},{2,3},{3,2},{16,17},{17,16},{18,19},{19,18},{4,5},{5,4... | collective-permute-start | bytes 13369352 | tf_op jit(solution)/shard_map/ppermute | solution.py:39
  57.2 21.4 %collective-permute-start.6 = (bf16[40,1024]{1,0:T(8,128)(2,1)S(1)}, bf16[40,1024]{1,0:T(8,128)(2,1)S(1)}, u32[]{:S(2)}, u32[]{:S(2)}) collective-permute-start(bf16[40,1024]{1,0:T(8,128)(2,1)S(1)} %get-tuple-element.7.own), channel_id=1, source_target_pairs={{0,256},{1,257},{2,258},{3,259},{16,272},{17,273},{18,274},{19,275... | collective-permute-start | bytes 245768 | tf_op jit(solution)/shard_map/ppermute | solution.py:39
  69.4 15.7 %collective-permute-start.5 = (bf16[40,1024]{1,0:T(8,128)(2,1)S(1)}, bf16[40,1024]{1,0:T(8,128)(2,1)S(1)}, u32[]{:S(2)}, u32[]{:S(2)}) collective-permute-start(bf16[40,1024]{1,0:T(8,128)(2,1)S(1)} %get-tuple-element.7.own), channel_id=1, source_target_pairs={{0,384},{1,385},{2,386},{3,387},{16,400},{17,401},{18,402},{19,403... | collective-permute-start | bytes 245768 | tf_op jit(solution)/shard_map/ppermute | solution.py:39
  71.3 13.8 %collective-permute-start.4 = (bf16[40,1024]{1,0:T(8,128)(2,1)S(1)}, bf16[40,1024]{1,0:T(8,128)(2,1)S(1)}, u32[]{:S(2)}, u32[]{:S(2)}) collective-permute-start(bf16[40,1024]{1,0:T(8,128)(2,1)S(1)} %get-tuple-element.7.own), channel_id=1, source_target_pairs={{0,128},{1,129},{2,130},{3,131},{16,144},{17,145},{18,146},{19,147... | collective-permute-start | bytes 245768 | tf_op jit(solution)/shard_map/ppermute | solution.py:39
  85.7 10.6 %collective-permute-start.9 = (bf16[136,1024]{1,0:T(8,128)(2,1)S(1)}, bf16[136,1024]{1,0:T(8,128)(2,1)S(1)}, u32[]{:S(2)}, u32[]{:S(2)}) collective-permute-start(bf16[136,1024]{1,0:T(8,128)(2,1)S(1)} %shard_map.43.far), channel_id=1, source_target_pairs={{0,32},{1,33},{2,34},{3,35},{16,48},{17,49},{18,50},{19,51},{4,36}... | collective-permute-start | bytes 835592 | tf_op jit(solution)/shard_map/ppermute | solution.py:39
  88.9 12.8 %collective-permute-start.8 = (bf16[136,1024]{1,0:T(8,128)(2,1)S(1)}, bf16[136,1024]{1,0:T(8,128)(2,1)S(1)}, u32[]{:S(2)}, u32[]{:S(2)}) collective-permute-start(bf16[136,1024]{1,0:T(8,128)(2,1)S(1)} %shard_map.43.far), channel_id=1, source_target_pairs={{0,64},{1,449},{2,66},{3,451},{16,80},{17,465},{18,82},{19,467},{4... | collective-permute-start | bytes 835592 | tf_op jit(solution)/shard_map/ppermute | solution.py:39
  93.4 13.0 %collective-permute-start.7 = (bf16[136,1024]{1,0:T(8,128)(2,1)S(1)}, bf16[136,1024]{1,0:T(8,128)(2,1)S(1)}, u32[]{:S(2)}, u32[]{:S(2)}) collective-permute-start(bf16[136,1024]{1,0:T(8,128)(2,1)S(1)} %shard_map.43.far), channel_id=1, source_target_pairs={{0,480},{1,481},{2,482},{3,483},{16,496},{17,497},{18,498},{19,499... | collective-permute-start | bytes 835592 | tf_op jit(solution)/shard_map/ppermute | solution.py:39

commit v4 on v3

--- a/solution.py
+++ b/solution.py
@@ -115,9 +115,9 @@
     far[KEYS:, :] = tail.astype(BF16)
 
 
-def keys_body(at, line, plus, minus, two, keys):
-    for k, ref in enumerate((line, plus, minus, two)):
-        keys[k] = ref[...]
+def rest_body(at, plus, minus, two, rest):
+    for k, ref in enumerate((plus, minus, two)):
+        rest[k] = ref[...]
 
 
 def anchors_body(at, far, ahead, across, behind, anchors):
@@ -171,17 +171,17 @@
                     totals[d][m] += part.reshape(n // 8, 8, n).sum(axis=0)
 
 
-def mine_body(at, keys, anchors, out):
+def mine_body(at, line, rest, anchors, out):
     totals = [[jnp.zeros((8, KEYS), F32) for _ in range(3)] for _ in range(4)]
-    scores_of(at, [keys.at[p] for p in range(4)], anchors, totals, True)
+    scores_of(at, (line, rest.at[0], rest.at[1], rest.at[2]), anchors, totals, True)
     for d in range(4):
         for k in range(3):
             out[d, k] = totals[d][k]
 
 
-def theirs_body(at, keys, anchors, before, out):
+def theirs_body(at, line, rest, anchors, before, out):
     totals = [[before[d, k] for k in range(3)] for d in range(4)]
-    scores_of(at, [keys.at[p] for p in range(4)], anchors, totals, False)
+    scores_of(at, (line, rest.at[0], rest.at[1], rest.at[2]), anchors, totals, False)
     for d in range(4):
         slot = (at[1] + d) % 4
         for k in range(3):
@@ -245,17 +245,18 @@
     behind = along_z(far, 1)
     ahead = along_z(far, -1)
 
-    (keys,) = call(keys_body, 4, (jax.ShapeDtypeStruct((4, 4, ROWS, D), BF16),))(at, line, *plane)
-    other_keys = other_core(keys)
+    (rest,) = call(rest_body, 3, (jax.ShapeDtypeStruct((3, 4, ROWS, D), BF16),))(at, *plane)
+    other_line = other_core(line)
+    other_rest = other_core(rest)
 
     column = jax.ShapeDtypeStruct((4 * KEYS + LAB, D), BF16)
     (anchors,) = call(anchors_body, 4, (column,))(at, far, ahead, across_near, behind)
-    (first,) = call(mine_body, 2, (jax.ShapeDtypeStruct((4, 3, 8, KEYS), F32),), (), 16)(
-        at, keys, anchors
+    (first,) = call(mine_body, 3, (jax.ShapeDtypeStruct((4, 3, 8, KEYS), F32),), (), 16)(
+        at, line, rest, anchors
     )
     (sums,) = call(
-        theirs_body, 3, (jax.ShapeDtypeStruct((Z, 3, 4, KEYS), F32),), (), 16
-    )(at, other_keys, anchors, first)
+        theirs_body, 4, (jax.ShapeDtypeStruct((Z, 3, 4, KEYS), F32),), (), 16
+    )(at, other_line, other_rest, anchors, first)
     arrived = swapped_to_all(sums, COLUMNS)
     own_loss, both = call(
         loss_body,

time: 153 us -> 154 us (level)
  starting transfers between devices: 48.5 us -> 50.5 us
    ppermute x10 -> x11, starting transfers between devices: 48.5 us -> 50.5 us  [moved(): lax.ppermute(block, 'd', [(device_at(*spot), device_at(*target(*spot))) f...]
    ppermute x10 -> x11, waiting for transfers between devices: 38 us -> 37.9 us  [moved(): lax.ppermute(block, 'd', [(device_at(*spot), device_at(*target(*spot))) f...]
  transfers between devices with their start and end apart: 10 -> 11, of which waited for: 6 -> 6; matrix products, arithmetic and copies ran while one was open for 0% -> 0% of each run, Pallas kernels for 3% -> 3%
where the time goes in v4:
time: 154 us; the launch traced here: 153 us
  starting transfers between devices  50.5 us (33%)
  blocking collectives  47.9 us (31%)
  waiting for transfers between devices  37.9 us (25%)
  Pallas kernels  11.2 us (7%)
  between operations  3.25 us (2%)
  local copies, waits for them, and re-layouts  2.19 us (1%)
    ppermute x11, starting transfers between devices, moved(): lax.ppermute(block, 'd', [(device_at(*spot), device_at(*target(*spot))) f...  50.5 us
    all_to_all x3, blocking collectives, swapped_to_all(): lax.all_to_all(blocks, 'd', 0, 0, tiled=True, axis_index_groups=groups)  47.9 us
    ppermute x11, waiting for transfers between devices, moved(): lax.ppermute(block, 'd', [(device_at(*spot), device_at(*target(*spot))) f...  37.9 us
    pallas_call x1, Pallas kernels, loss_of(): call(theirs_body, 4, (jax.ShapeDtypeStruct((Z, 3, 4, KEYS), F32),), (), 16)  3.68 us
    pallas_call x1, Pallas kernels, loss_of(): call(mine_body, 3, (jax.ShapeDtypeStruct((4, 3, 8, KEYS), F32),), (), 16)  3.67 us
  transfers between devices with their start and end apart: 11, of which 6 were waited for; matrix products, arithmetic and copies ran while one was open for 0% of the time, Pallas kernels for 3%

profile of v4, /device:TPU:1, one launch (start us, length us, event | category | flops | bytes accessed | tf_op | source)
XLA Modules:
  0.0 153.0 jit_solution(3223280398585468600)
XLA Ops:
  0.7 0.1 pad_add_fusion.at
  0.8 0.0 copy-start
  0.8 0.9 copy-done
  1.8 0.0 copy-start.1
  1.8 0.7 copy-done.1
  2.4 0.7 shard_map.41
  3.1 15.2 %all_to_all.15.line = bf16[4,136,1024]{2,1,0:T(8,128)(2,1)S(1)} all-to-all(bf16[4,136,1024]{2,1,0:T(8,128)(2,1)S(1)} %get-tuple-element.6), channel_id=1, replica_groups={{0,4,8,12},{2,6,10,14},{16,20,24,28},{18,22,26,30},{32,36,40,44},{34,38..., dimensions={0} | all-to-all | bytes 2228224 | tf_op jit(solution)/shard_map/all_to_all | solution.py:61
  18.3 4.3 %collective-permute-start.3 = (bf16[4,136,1024]{2,1,0:T(8,128)(2,1)S(1)}, bf16[4,136,1024]{2,1,0:T(8,128)(2,1)S(1)}, u32[]{:S(2)}, u32[]{:S(2)}) collective-permute-start(bf16[4,136,1024]{2,1,0:T(8,128)(2,1)S(1)} %all_to_all.15.line), channel_id=1, source_target_pairs={{0,16},{1,9},{2,18},{3,11},{16,0},{17,25},{18,2},{19,27},{4,20},{5... | collective-permute-start | bytes 3342344 | tf_op jit(solution)/shard_map/ppermute | solution.py:39
  22.7 2.8 %collective-permute-start.2 = (bf16[4,136,1024]{2,1,0:T(8,128)(2,1)S(1)}, bf16[4,136,1024]{2,1,0:T(8,128)(2,1)S(1)}, u32[]{:S(2)}, u32[]{:S(2)}) collective-permute-start(bf16[4,136,1024]{2,1,0:T(8,128)(2,1)S(1)} %all_to_all.15.line), channel_id=1, source_target_pairs={{0,18},{1,13},{2,0},{3,15},{16,2},{17,29},{18,16},{19,31},{4,22},{... | collective-permute-start | bytes 3342344 | tf_op jit(solution)/shard_map/ppermute | solution.py:39
  25.5 2.5 %collective-permute-start.1 = (bf16[4,136,1024]{2,1,0:T(8,128)(2,1)S(1)}, bf16[4,136,1024]{2,1,0:T(8,128)(2,1)S(1)}, u32[]{:S(2)}, u32[]{:S(2)}) collective-permute-start(bf16[4,136,1024]{2,1,0:T(8,128)(2,1)S(1)} %all_to_all.15.line), channel_id=1, source_target_pairs={{0,2},{1,5},{2,16},{3,7},{16,18},{17,21},{18,0},{19,23},{4,6},{5,9... | collective-permute-start | bytes 3342344 | tf_op jit(solution)/shard_map/ppermute | solution.py:39
  28.0 8.4 %collective-permute-done.3.two = bf16[4,136,1024]{2,1,0:T(8,128)(2,1)S(1)} collective-permute-done((bf16[4,136,1024]{2,1,0:T(8,128)(2,1)S(1)}, bf16[4,136,1024]{2,1,0:T(8,128)(2,1)S(1)}, u32[]{:S(2)}, u32[]{:S(2)}) %collective-permute-start.3) | collective-permute-done | bytes 1114144 | tf_op jit(solution)/shard_map/ppermute | solution.py:39
  36.4 12.0 %collective-permute-done.2.minus = bf16[4,136,1024]{2,1,0:T(8,128)(2,1)S(1)} collective-permute-done((bf16[4,136,1024]{2,1,0:T(8,128)(2,1)S(1)}, bf16[4,136,1024]{2,1,0:T(8,128)(2,1)S(1)}, u32[]{:S(2)}, u32[]{:S(2)}) %collective-permute-start.2) | collective-permute-done | bytes 1114144 | tf_op jit(solution)/shard_map/ppermute | solution.py:39
  48.4 0.0 collective-permute-done.1.plus
  48.4 0.8 shard_map.42.rest
  49.2 7.9 %collective-permute-start.4 = (bf16[3,4,136,1024]{3,2,1,0:T(8,128)(2,1)S(1)}, bf16[3,4,136,1024]{3,2,1,0:T(8,128)(2,1)S(1)}, u32[]{:S(2)}, u32[]{:S(2)}) collective-permute-start(bf16[3,4,136,1024]{3,2,1,0:T(8,128)(2,1)S(1)} %shard_map.42.rest), channel_id=1, source_target_pairs={{0,1},{1,0},{2,3},{3,2},{16,17},{17,16},{18,19},{19,18},{4,5},{5,4... | collective-permute-start | bytes 10027016 | tf_op jit(solution)/shard_map/ppermute | solution.py:39
  57.1 1.9 %collective-permute-start = (bf16[4,136,1024]{2,1,0:T(8,128)(2,1)S(1)}, bf16[4,136,1024]{2,1,0:T(8,128)(2,1)S(1)}, u32[]{:S(2)}, u32[]{:S(2)}) collective-permute-start(bf16[4,136,1024]{2,1,0:T(8,128)(2,1)S(1)} %all_to_all.15.line), channel_id=1, source_target_pairs={{0,1},{1,0},{2,3},{3,2},{16,17},{17,16},{18,19},{19,18},{4,5},{5,4... | collective-permute-start | bytes 3342344 | tf_op jit(solution)/shard_map/ppermute | solution.py:39
  59.1 12.2 %collective-permute-start.7 = (bf16[40,1024]{1,0:T(8,128)(2,1)S(1)}, bf16[40,1024]{1,0:T(8,128)(2,1)S(1)}, u32[]{:S(2)}, u32[]{:S(2)}) collective-permute-start(bf16[40,1024]{1,0:T(8,128)(2,1)S(1)} %get-tuple-element.7.own), channel_id=1, source_target_pairs={{0,256},{1,257},{2,258},{3,259},{16,272},{17,273},{18,274},{19,275... | collective-permute-start | bytes 245768 | tf_op jit(solution)/shard_map/ppermute | solution.py:39
  71.2 1.9 %collective-permute-start.6 = (bf16[40,1024]{1,0:T(8,128)(2,1)S(1)}, bf16[40,1024]{1,0:T(8,128)(2,1)S(1)}, u32[]{:S(2)}, u32[]{:S(2)}) collective-permute-start(bf16[40,1024]{1,0:T(8,128)(2,1)S(1)} %get-tuple-element.7.own), channel_id=1, source_target_pairs={{0,384},{1,385},{2,386},{3,387},{16,400},{17,401},{18,402},{19,403... | collective-permute-start | bytes 245768 | tf_op jit(solution)/shard_map/ppermute | solution.py:39
  73.2 7.3 %collective-permute-start.5 = (bf16[40,1024]{1,0:T(8,128)(2,1)S(1)}, bf16[40,1024]{1,0:T(8,128)(2,1)S(1)}, u32[]{:S(2)}, u32[]{:S(2)}) collective-permute-start(bf16[40,1024]{1,0:T(8,128)(2,1)S(1)} %get-tuple-element.7.own), channel_id=1, source_target_pairs={{0,128},{1,129},{2,130},{3,131},{16,144},{17,145},{18,146},{19,147... | collective-permute-start | bytes 245768 | tf_op jit(solution)/shard_map/ppermute | solution.py:39
  80.4 0.0 collective-permute-done.7.across
  80.5 6.4 %collective-permute-done.6.after = bf16[40,1024]{1,0:T(8,128)(2,1)S(1)} collective-permute-done((bf16[40,1024]{1,0:T(8,128)(2,1)S(1)}, bf16[40,1024]{1,0:T(8,128)(2,1)S(1)}, u32[]{:S(2)}, u32[]{:S(2)}) %collective-permute-start.6) | collective-permute-done | bytes 81952 | tf_op jit(solution)/shard_map/ppermute | solution.py:39
  86.9 0.0 collective-permute-done.5.before
  86.9 0.6 shard_map.43.far
  87.5 3.3 %collective-permute-start.10 = (bf16[136,1024]{1,0:T(8,128)(2,1)S(1)}, bf16[136,1024]{1,0:T(8,128)(2,1)S(1)}, u32[]{:S(2)}, u32[]{:S(2)}) collective-permute-start(bf16[136,1024]{1,0:T(8,128)(2,1)S(1)} %shard_map.43.far), channel_id=1, source_target_pairs={{0,32},{1,33},{2,34},{3,35},{16,48},{17,49},{18,50},{19,51},{4,36}... | collective-permute-start | bytes 835592 | tf_op jit(solution)/shard_map/ppermute | solution.py:39
  90.8 4.4 %collective-permute-start.9 = (bf16[136,1024]{1,0:T(8,128)(2,1)S(1)}, bf16[136,1024]{1,0:T(8,128)(2,1)S(1)}, u32[]{:S(2)}, u32[]{:S(2)}) collective-permute-start(bf16[136,1024]{1,0:T(8,128)(2,1)S(1)} %shard_map.43.far), channel_id=1, source_target_pairs={{0,64},{1,449},{2,66},{3,451},{16,80},{17,465},{18,82},{19,467},{4... | collective-permute-start | bytes 835592 | tf_op jit(solution)/shard_map/ppermute | solution.py:39
  95.2 1.9 %collective-permute-start.8 = (bf16[136,1024]{1,0:T(8,128)(2,1)S(1)}, bf16[136,1024]{1,0:T(8,128)(2,1)S(1)}, u32[]{:S(2)}, u32[]{:S(2)}) collective-permute-start(bf16[136,1024]{1,0:T(8,128)(2,1)S(1)} %shard_map.43.far), channel_id=1, source_target_pairs={{0,480},{1,481},{2,482},{3,483},{16,496},{17,497},{18,498},{19,499... | collective-permute-start | bytes 835592 | tf_op jit(solution)/shard_map/ppermute | solution.py:39
  97.1 1.0 collective-permute-done.10.behind
  98.1 5.3 %collective-permute-done.9.across = bf16[136,1024]{1,0:T(8,128)(2,1)S(1)} collective-permute-done((bf16[136,1024]{1,0:T(8,128)(2,1)S(1)}, bf16[136,1024]{1,0:T(8,128)(2,1)S(1)}, u32[]{:S(2)}, u32[]{:S(2)}) %collective-permute-start.9) | collective-permute-done | bytes 278560 | tf_op jit(solution)/shard_map/ppermute | solution.py:39
  103.4 4.8 %collective-permute-done.8.ahead = bf16[136,1024]{1,0:T(8,128)(2,1)S(1)} collective-permute-done((bf16[136,1024]{1,0:T(8,128)(2,1)S(1)}, bf16[136,1024]{1,0:T(8,128)(2,1)S(1)}, u32[]{:S(2)}, u32[]{:S(2)}) %collective-permute-start.8) | collective-permute-done | bytes 278560 | tf_op jit(solution)/shard_map/ppermute | solution.py:39
  108.2 0.6 shard_map.44.anchors
  108.8 3.7 %shard_map.45.before = f32[4,3,8,128]{3,2,1,0:T(8,128)S(1)} custom-call(s32[4]{0:T(128)S(1)} %pad_add_fusion.at, bf16[4,136,1024]{2,1,0:T(8,128)(2,1)S(1)} %all_to_all.15.line, bf16[3,4,136,1024]{3,2,1,0:T(8,128)(2,1)S(1)} %shard_map.42.rest, bf16[520,1024]{1,0:T(8,128)(2,1)S(1)} %shard_map.44.anchors), custom_call_target="tpu_custom_call" | custom-call | tf_op jit(solution)/shard_map/pallas_call | solution.py:254
  112.5 0.0 collective-permute-done.line
  112.5 0.0 collective-permute-done.4.rest
  112.5 3.7 %shard_map.46 = f32[16,3,4,128]{3,2,1,0:T(4,128)S(1)} custom-call(s32[4]{0:T(128)S(1)} %pad_add_fusion.at, bf16[4,136,1024]{2,1,0:T(8,128)(2,1)S(1)} %collective-permute-done.line, bf16[3,4,136,1024]{3,2,1,0:T(8,128)(2,1)S(1)} %collective-permute-done.4.rest, bf16[520,1024]{1,0:T(8,128)(2,1)S(1)} %shard_map.44.anchors, f32[4,3,8,128]{3,2,1,0:T(8,128)S(1)} %shard_map.45.before), custom_call_target="tpu_custom_call" | custom-call | tf_op jit(solution)/shard_map/pallas_call | solution.py:257
  116.2 20.5 %all_to_all.16.arrived = f32[16,3,4,128]{3,2,1,0:T(4,128)S(1)} all-to-all(f32[16,3,4,128]{3,2,1,0:T(4,128)S(1)} %shard_map.46), channel_id=1, replica_groups={{0,32,64,96,128,160,192,224,256,288,320,352,384,416,448,480},{1,33,65,9..., dimensions={0} | all-to-all | bytes 196608 | tf_op jit(solution)/shard_map/all_to_all | solution.py:61
  136.7 1.2 shard_map.47
  137.8 12.2 %all_to_all.17 = f32[32,1,128]{2,1,0:T(1,128)S(1)} all-to-all(f32[32,1,128]{2,1,0:T(1,128)S(1)} %get-tuple-element.9), channel_id=1, replica_groups={{0,1,2,3,16,17,18,19,4,5,6,7,20,21,22,23,8,9,10,11,24,25,26,27,12,13,14..., dimensions={0} | all-to-all | bytes 32768 | tf_op jit(solution)/shard_map/all_to_all | solution.py:61
  150.0 0.1 reduce_sum.11
  150.1 0.6 fusion
Async XLA Ops:
  0.8 1.0 copy-start
  1.8 0.7 copy-start.1
  18.3 18.1 %collective-permute-start.3 = (bf16[4,136,1024]{2,1,0:T(8,128)(2,1)S(1)}, bf16[4,136,1024]{2,1,0:T(8,128)(2,1)S(1)}, u32[]{:S(2)}, u32[]{:S(2)}) collective-permute-start(bf16[4,136,1024]{2,1,0:T(8,128)(2,1)S(1)} %all_to_all.15.line), channel_id=1, source_target_pairs={{0,16},{1,9},{2,18},{3,11},{16,0},{17,25},{18,2},{19,27},{4,20},{5... | collective-permute-start | bytes 3342344 | tf_op jit(solution)/shard_map/ppermute | solution.py:39
  22.7 25.7 %collective-permute-start.2 = (bf16[4,136,1024]{2,1,0:T(8,128)(2,1)S(1)}, bf16[4,136,1024]{2,1,0:T(8,128)(2,1)S(1)}, u32[]{:S(2)}, u32[]{:S(2)}) collective-permute-start(bf16[4,136,1024]{2,1,0:T(8,128)(2,1)S(1)} %all_to_all.15.line), channel_id=1, source_target_pairs={{0,18},{1,13},{2,0},{3,15},{16,2},{17,29},{18,16},{19,31},{4,22},{... | collective-permute-start | bytes 3342344 | tf_op jit(solution)/shard_map/ppermute | solution.py:39
  25.5 23.0 %collective-permute-start.1 = (bf16[4,136,1024]{2,1,0:T(8,128)(2,1)S(1)}, bf16[4,136,1024]{2,1,0:T(8,128)(2,1)S(1)}, u32[]{:S(2)}, u32[]{:S(2)}) collective-permute-start(bf16[4,136,1024]{2,1,0:T(8,128)(2,1)S(1)} %all_to_all.15.line), channel_id=1, source_target_pairs={{0,2},{1,5},{2,16},{3,7},{16,18},{17,21},{18,0},{19,23},{4,6},{5,9... | collective-permute-start | bytes 3342344 | tf_op jit(solution)/shard_map/ppermute | solution.py:39
  49.2 63.3 %collective-permute-start.4 = (bf16[3,4,136,1024]{3,2,1,0:T(8,128)(2,1)S(1)}, bf16[3,4,136,1024]{3,2,1,0:T(8,128)(2,1)S(1)}, u32[]{:S(2)}, u32[]{:S(2)}) collective-permute-start(bf16[3,4,136,1024]{3,2,1,0:T(8,128)(2,1)S(1)} %shard_map.42.rest), channel_id=1, source_target_pairs={{0,1},{1,0},{2,3},{3,2},{16,17},{17,16},{18,19},{19,18},{4,5},{5,4... | collective-permute-start | bytes 10027016 | tf_op jit(solution)/shard_map/ppermute | solution.py:39
  57.1 55.3 %collective-permute-start = (bf16[4,136,1024]{2,1,0:T(8,128)(2,1)S(1)}, bf16[4,136,1024]{2,1,0:T(8,128)(2,1)S(1)}, u32[]{:S(2)}, u32[]{:S(2)}) collective-permute-start(bf16[4,136,1024]{2,1,0:T(8,128)(2,1)S(1)} %all_to_all.15.line), channel_id=1, source_target_pairs={{0,1},{1,0},{2,3},{3,2},{16,17},{17,16},{18,19},{19,18},{4,5},{5,4... | collective-permute-start | bytes 3342344 | tf_op jit(solution)/shard_map/ppermute | solution.py:39
  59.1 21.4 %collective-permute-start.7 = (bf16[40,1024]{1,0:T(8,128)(2,1)S(1)}, bf16[40,1024]{1,0:T(8,128)(2,1)S(1)}, u32[]{:S(2)}, u32[]{:S(2)}) collective-permute-start(bf16[40,1024]{1,0:T(8,128)(2,1)S(1)} %get-tuple-element.7.own), channel_id=1, source_target_pairs={{0,256},{1,257},{2,258},{3,259},{16,272},{17,273},{18,274},{19,275... | collective-permute-start | bytes 245768 | tf_op jit(solution)/shard_map/ppermute | solution.py:39
  71.2 15.7 %collective-permute-start.6 = (bf16[40,1024]{1,0:T(8,128)(2,1)S(1)}, bf16[40,1024]{1,0:T(8,128)(2,1)S(1)}, u32[]{:S(2)}, u32[]{:S(2)}) collective-permute-start(bf16[40,1024]{1,0:T(8,128)(2,1)S(1)} %get-tuple-element.7.own), channel_id=1, source_target_pairs={{0,384},{1,385},{2,386},{3,387},{16,400},{17,401},{18,402},{19,403... | collective-permute-start | bytes 245768 | tf_op jit(solution)/shard_map/ppermute | solution.py:39
  73.2 13.7 %collective-permute-start.5 = (bf16[40,1024]{1,0:T(8,128)(2,1)S(1)}, bf16[40,1024]{1,0:T(8,128)(2,1)S(1)}, u32[]{:S(2)}, u32[]{:S(2)}) collective-permute-start(bf16[40,1024]{1,0:T(8,128)(2,1)S(1)} %get-tuple-element.7.own), channel_id=1, source_target_pairs={{0,128},{1,129},{2,130},{3,131},{16,144},{17,145},{18,146},{19,147... | collective-permute-start | bytes 245768 | tf_op jit(solution)/shard_map/ppermute | solution.py:39
  87.5 10.6 %collective-permute-start.10 = (bf16[136,1024]{1,0:T(8,128)(2,1)S(1)}, bf16[136,1024]{1,0:T(8,128)(2,1)S(1)}, u32[]{:S(2)}, u32[]{:S(2)}) collective-permute-start(bf16[136,1024]{1,0:T(8,128)(2,1)S(1)} %shard_map.43.far), channel_id=1, source_target_pairs={{0,32},{1,33},{2,34},{3,35},{16,48},{17,49},{18,50},{19,51},{4,36}... | collective-permute-start | bytes 835592 | tf_op jit(solution)/shard_map/ppermute | solution.py:39
  90.8 12.6 %collective-permute-start.9 = (bf16[136,1024]{1,0:T(8,128)(2,1)S(1)}, bf16[136,1024]{1,0:T(8,128)(2,1)S(1)}, u32[]{:S(2)}, u32[]{:S(2)}) collective-permute-start(bf16[136,1024]{1,0:T(8,128)(2,1)S(1)} %shard_map.43.far), channel_id=1, source_target_pairs={{0,64},{1,449},{2,66},{3,451},{16,80},{17,465},{18,82},{19,467},{4... | collective-permute-start | bytes 835592 | tf_op jit(solution)/shard_map/ppermute | solution.py:39
  95.2 13.0 %collective-permute-start.8 = (bf16[136,1024]{1,0:T(8,128)(2,1)S(1)}, bf16[136,1024]{1,0:T(8,128)(2,1)S(1)}, u32[]{:S(2)}, u32[]{:S(2)}) collective-permute-start(bf16[136,1024]{1,0:T(8,128)(2,1)S(1)} %shard_map.43.far), channel_id=1, source_target_pairs={{0,480},{1,481},{2,482},{3,483},{16,496},{17,497},{18,498},{19,499... | collective-permute-start | bytes 835592 | tf_op jit(solution)/shard_map/ppermute | solution.py:39
